TPU v7x, 32 devices: a whole 2x2x4 slice. The times are simulated.
32 devices in a mesh: pairs: 2 (over x), ctx: 16 (over z, y, core).
Axes of the slice: x: 2, y: 2, z: 4, core: 2. Of those that a mesh axis runs over, the one named last changes fastest.
Arguments:
- prompt_keys: bfloat16 [1024, 512], P(('pairs', 'ctx')), parts along dimension 0, may hold values from -4 to 4
- prompt_values: bfloat16 [1024, 512], P(('pairs', 'ctx')), parts along dimension 0, may hold values from -6 to 6
- queries: bfloat16 [4, 768, 4096], P('pairs', 'ctx'), parts along dimension 0, may hold values from -100 to 100
- resp_keys: bfloat16 [4, 768, 512], P('pairs', 'ctx'), parts along dimension 0, may hold values from -6 to 6
- resp_values: bfloat16 [4, 768, 512], P('pairs', 'ctx'), parts along dimension 0, may hold values from -6 to 6
- cotangent: bfloat16 [4, 768, 4096], P('pairs', 'ctx'), parts along dimension 0, may hold values from -48 to 48
- lengths: int32 [4], P('pairs'), parts along dimension 0, may hold values from 192 to 768, as said below
Outputs:
- grad_queries: float32 [4, 768, 4096], P('pairs', 'ctx'), parts along dimension 0
- grad_resp_keys: float32 [4, 768, 512], P('pairs', 'ctx'), parts along dimension 0
- grad_resp_values: float32 [4, 768, 512], P('pairs', 'ctx'), parts along dimension 0
- grad_prompt_keys: float32 [1024, 512], P(('pairs', 'ctx')), parts along dimension 0
- grad_prompt_values: float32 [1024, 512], P(('pairs', 'ctx')), parts along dimension 0
There are 2 independent parts, one for each index of `pairs`. A program takes and returns all parts, laid end to end along the dimension named above; each array names one. Nothing has to cross between parts.
Inputs may be any that keep to these rules, and one draw needn't show every extreme that they name: `lengths`: in every pair one of the two responses has all 768 rows live.
All inputs are finite; a program needn't handle non-finite values.
Results may differ from a plain program's by a relative error of at most 0.005.
Values may be sent and summed in bfloat16 or wider, within the bound.
A program may use at most 128 MiB of HBM per device.

v0:
```python
import functools

import jax
import jax.numpy as jnp
from jax import lax
from jax.experimental import pallas as pl
from jax.experimental.pallas import tpu as pltpu
from jax.sharding import PartitionSpec as P

HEAD_DIM = 128
SCALE = HEAD_DIM ** (-0.5)
LOG2E = 1.4426950408889634
MIB = 1024 * 1024
TICKS = 7


def chip_of(pos, n):
    high = pos // (n // 2)
    return (1 - high) * (2 * pos) + high * (2 * (n - 1 - pos) + 1)


def place(n):
    me = lax.axis_index("ctx")
    core, chip = me % 2, me // 2
    odd = chip % 2
    pos = (1 - odd) * (chip // 2) + odd * (n - 1 - chip // 2)
    partner = 2 * chip + 1 - core
    right = 2 * chip_of((pos + 1) % n, n) + core
    left = 2 * chip_of((pos + n - 1) % n, n) + core
    return core, chip, pos, partner, (right, left)


def greet(partner, sides):
    barrier = pltpu.get_barrier_semaphore()
    for other in (partner,) + sides:
        pl.semaphore_signal(
            barrier, inc=1, device_id={"ctx": other}, device_id_type=pl.DeviceIdType.MESH
        )
    pl.semaphore_wait(barrier, 3)


def steps_of(n):
    far, near = n // 2, n - 1 - n // 2
    return ((far, near), (near, far))


def remote(src, dst, send, recv, device):
    return pltpu.make_async_remote_copy(
        src_ref=src,
        dst_ref=dst,
        send_sem=send,
        recv_sem=recv,
        device_id={"ctx": device},
        device_id_type=pl.DeviceIdType.MESH,
    )


def fused_kernel(
    n, block, lengths, pk, pv, rk, rv, q, u,
    gq, grk, grv, gpk, gpv,
    kp, kr, qh, uh, qs, us, s_buf, d_buf, qt_buf, m_buf, l_buf, e_buf,
    tp, tr, sp, sr, rp, rr, fp, fr, dq,
    gsend, grecv, ssend, srecv, isend, irecv, ilocal, qsend, qrecv, qlocal,
    osend, orecv, olocal,
):
    core, chip, pos, partner, sides = place(n)
    prows, rrows = pk.shape[0], rk.shape[1]
    wide = q.shape[2] // 2
    heads = kp.shape[1]
    group = wide // HEAD_DIM // heads
    units = [(k, b) for k in range(heads) for b in range(2)]
    hops = steps_of(n)
    flows = ((0, 0), (1, 1), (0, 1), (1, 0))
    inputs = ((pk, rk), (pv, rv))
    outputs = ((gpk, grk), (gpv, grv))

    def head_columns(owner, k):
        return pl.ds(pl.multiple_of((owner * heads + k) * HEAD_DIM, HEAD_DIM), HEAD_DIM)

    def parts_in(unit):
        return (0, 1) if units[unit][1] == 0 else (1,)

    def parts_out(unit):
        return (1,) if units[unit][1] == 0 else (0, 1)

    def rows_of(where, size):
        return pl.ds(pl.multiple_of(where * size, 16), size)

    def gathered(kind, unit, part, rows):
        k, b = units[unit]
        return kp.at[kind, k, rows, :] if part == 0 else kr.at[kind, k, b, rows, :]

    def given(kind, unit, part, cols):
        ref = inputs[kind][part]
        return ref.at[:, cols] if part == 0 else ref.at[units[unit][1], :, cols]

    greet(partner, sides)
    entries = []
    for unit in range(len(units)):
        k = units[unit][0]
        for part in parts_in(unit):
            size = prows if part == 0 else rrows
            own = rows_of(chip * 2 + core, size)
            for kind in range(2):
                at = (kind, unit, part)
                away = remote(
                    given(kind, unit, part, head_columns(1 - core, k)),
                    gathered(kind, unit, part, own), isend.at[at], irecv.at[at], partner,
                )
                away.start()
                stay = pltpu.make_async_copy(
                    given(kind, unit, part, head_columns(core, k)),
                    gathered(kind, unit, part, own), ilocal.at[at],
                )
                stay.start()
                entries.append((unit, away, stay))
    wide_own = pl.ds(pl.multiple_of(core * wide, wide), wide)
    wide_far = pl.ds(pl.multiple_of((1 - core) * wide, wide), wide)
    query_moves = []
    for i, (src, dst) in enumerate(((q, qh), (u, uh))):
        away = remote(src.at[:, :, wide_far], dst.at[1], qsend.at[i], qrecv.at[i], partner)
        away.start()
        stay = pltpu.make_async_copy(src.at[:, :, wide_own], dst.at[0], qlocal.at[i])
        stay.start()
        query_moves += [away, stay]

    moved = {}

    def pull(unit, t):
        if t == 1:
            for owner, away, stay in entries:
                if owner == unit:
                    away.wait_recv()
                    stay.wait()
        for part in parts_in(unit):
            size = 2 * (prows if part == 0 else rrows)
            for way, kind in flows:
                if t > hops[way][kind]:
                    continue
                if t > 1:
                    moved[unit, t - 1, part, way, kind].wait_recv()
                origin = (pos + n - (t - 1)) % n if way == 0 else (pos + t - 1) % n
                ref = gathered(kind, unit, part, rows_of(chip_of(origin, n), size))
                at = (way, kind, unit, part, t - 1)
                copy = remote(ref, ref, gsend.at[at], grecv.at[at], sides[way])
                copy.start()
                moved[unit, t, part, way, kind] = copy

    def pulled(unit):
        for part in parts_in(unit):
            for way, kind in flows:
                moved[unit, hops[way][kind], part, way, kind].wait_recv()

    sent = {}

    def term(kind, unit, part, where):
        k, b = units[unit]
        if part == 0:
            return tp[kind, k, rows_of(where, 2 * prows), :]
        return tr[kind, k, b, rows_of(where, 2 * rrows), :]

    def slot(bufs, part, way, kind, unit, t):
        k = units[unit][0]
        if part == 0:
            return bufs[0].at[way, kind, k, t - 1]
        return bufs[1].at[way, kind, unit, t - 1]

    def push(unit, t, part):
        for way, kind in flows:
            total = hops[way][kind]
            if t > total:
                continue
            away = total - t + 1
            target = (pos + away) % n if way == 0 else (pos + n - away) % n
            value = term(kind, unit, part, chip_of(target, n))
            if t > 1:
                sent[unit, t - 1, part, way, kind].wait_recv()
                value = value + slot((rp, rr), part, way, kind, unit, t - 1)[...].astype(jnp.float32)
            src = slot((sp, sr), part, way, kind, unit, t)
            src[...] = value.astype(jnp.bfloat16)
            at = (way, kind, unit, part, t - 1)
            copy = remote(
                src, slot((rp, rr), part, way, kind, unit, t), ssend.at[at], srecv.at[at], sides[way]
            )
            copy.start()
            sent[unit, t, part, way, kind] = copy

    outgoing = []

    def finish(unit, part):
        k, b = units[unit]
        size = prows if part == 0 else rrows
        for kind in range(2):
            value = term(kind, unit, part, chip)
            for way in range(2):
                last = hops[way][kind]
                sent[unit, last, part, way, kind].wait_recv()
                value = value + slot((rp, rr), part, way, kind, unit, last)[...].astype(jnp.float32)
            final = fp.at[kind, k] if part == 0 else fr.at[kind, k, b]
            final[...] = value
            out = outputs[kind][part]
            cols = head_columns(core, k)
            dst = out.at[:, cols] if part == 0 else out.at[b, :, cols]
            at = (kind, unit, part)
            away = remote(
                final.at[rows_of(1 - core, size), :], dst, osend.at[at], orecv.at[at], partner
            )
            away.start()
            stay = pltpu.make_async_copy(final.at[rows_of(core, size), :], dst, olocal.at[at])
            stay.start()
            outgoing.extend((away, stay))

    half = group * rrows
    lanes = 2 * half
    prompt_blocks = kp.shape[2] // block
    resp_blocks = kr.shape[3] // block
    base = chip * 2 * rrows
    factor = SCALE * LOG2E
    lane = lax.broadcasted_iota(jnp.int32, (1, lanes), 1)
    row_of = lax.rem(lane, rrows)
    positions = base + row_of + rrows * jnp.where(lane < half, core, 1 - core)
    key_iota = lax.broadcasted_iota(jnp.int32, (block, 1), 0)
    row_iota = lax.broadcasted_iota(jnp.int32, (rrows, 1), 0)
    nt = (((1,), (1,)), ((), ()))

    def key_rows(j):
        return pl.ds(pl.multiple_of(j * block, block), block)

    def compute(unit, ticks):
        k, b = units[unit]
        length = lengths[b]
        for source in range(2):
            owner = core if source == 0 else 1 - core
            live = base + owner * rrows + row_iota < length
            for g in range(group):
                cols = pl.ds((k * group + g) * HEAD_DIM, HEAD_DIM)
                at = pl.ds(source * half + g * rrows, rrows)
                qs[at, :] = qh[source, b, :, cols]
                rows = uh[source, b, :, cols]
                us[at, :] = jnp.where(live, rows, jnp.zeros_like(rows))
        m_buf[...] = jnp.full_like(m_buf, -jnp.inf)
        l_buf[...] = jnp.zeros_like(l_buf)
        e_buf[...] = jnp.zeros_like(e_buf)
        qt_buf[...] = jnp.zeros_like(qt_buf)
        ticks(0)

        def scores(keys, at, j, causal):
            s = lax.dot_general(keys, qs[...], nt, preferred_element_type=jnp.float32)
            if causal:
                s = jnp.where(key_iota + j * block <= positions, s, -jnp.inf)
            s_buf[at, :] = s
            m_buf[...] = jnp.maximum(m_buf[...], jnp.max(s, axis=0, keepdims=True))

        @pl.loop(0, prompt_blocks, unroll=True)
        def _(j):
            scores(kp[0, k, key_rows(j), :], key_rows(j), j, False)

        ticks(1)

        @pl.loop(0, resp_blocks, unroll=True)
        def _(j):
            scores(kr[0, k, b, key_rows(j), :], key_rows(prompt_blocks + j), j, True)

        ticks(2)
        shift = m_buf[...] * factor

        def weights(vals, at):
            p = jnp.exp2(s_buf[at, :] * factor - shift)
            d = lax.dot_general(vals, us[...], nt, preferred_element_type=jnp.float32)
            l_buf[...] += jnp.sum(p, axis=0, keepdims=True)
            e_buf[...] += jnp.sum(p * d, axis=0, keepdims=True)
            s_buf[at, :] = p
            d_buf[at, :] = d

        @pl.loop(0, prompt_blocks, unroll=True)
        def _(j):
            weights(kp[1, k, key_rows(j), :], key_rows(j))

        ticks(3)

        @pl.loop(0, resp_blocks, unroll=True)
        def _(j):
            weights(kr[1, k, b, key_rows(j), :], key_rows(prompt_blocks + j))

        ticks(4)
        inverse = 1.0 / l_buf[...]
        delta = e_buf[...] * inverse

        def grads(keys, at):
            p = s_buf[at, :] * inverse
            ds = (p * (d_buf[at, :] - delta)).astype(jnp.bfloat16)
            dv = jnp.dot(p.astype(jnp.bfloat16), us[...], preferred_element_type=jnp.float32)
            dk = jnp.dot(ds, qs[...], preferred_element_type=jnp.float32) * SCALE
            qt_buf[...] += jnp.dot(keys.T, ds, preferred_element_type=jnp.float32)
            return dk, dv

        @pl.loop(0, prompt_blocks, unroll=True)
        def _(j):
            at = key_rows(j)
            pair = grads(kp[0, k, at, :], at)
            for kind in range(2):
                if b == 0:
                    tp[kind, k, at, :] = pair[kind]
                else:
                    tp[kind, k, at, :] += pair[kind]

        ticks(5)

        @pl.loop(0, resp_blocks, unroll=True)
        def _(j):
            at = key_rows(j)
            pair = grads(kr[0, k, b, at, :], key_rows(prompt_blocks + j))
            for kind in range(2):
                tr[kind, k, b, at, :] = pair[kind]

        ticks(6)
        result = qt_buf[...].T * SCALE
        for source in range(2):
            for g in range(group):
                start = source * half + g * rrows
                dq[source, b, :, pl.ds((k * group + g) * HEAD_DIM, HEAD_DIM)] = result[
                    start : start + rrows
                ]
        span = group * HEAD_DIM
        cols = pl.ds(k * span, span)
        to = pl.ds(pl.multiple_of(core * wide + k * span, span), span)
        i = 2 + unit
        away = remote(dq.at[1, b, :, cols], gq.at[b, :, to], qsend.at[i], qrecv.at[i], partner)
        away.start()
        stay = pltpu.make_async_copy(dq.at[0, b, :, cols], gq.at[b, :, to], qlocal.at[i])
        stay.start()
        outgoing.extend((away, stay))

    last = len(units) - 1
    far = n // 2
    pulls = [(w - t + 1, t) for w in range(last + far) for t in range(1, far + 1) if 0 <= w - t + 1 <= last]
    pulls.sort(key=lambda hop: (2 * hop[0] + hop[1], hop[1]))

    def advance(count):
        for _ in range(min(count, len(pulls))):
            pull(*pulls.pop(0))

    first = pulls.index((0, far)) + 1
    advance(1)
    for copy in query_moves:
        copy.wait()
    advance(first - 1)
    pulled(0)
    per_tick = -(-len(pulls) // 12)
    due = {}
    for unit in range(last):
        for t in range(1, far + 1):
            when = (unit + 1) * TICKS + (t - 1) * 12 // far
            due.setdefault(min(when, (last + 1) * TICKS), []).append((unit, t))

    def push_all(unit, t):
        for part in reversed(parts_out(unit)):
            push(unit, t, part)
        if t == far:
            closing.append(unit)

    closing = []
    for unit in range(last + 1):

        def ticks(at, unit=unit):
            for which, t in due.get(unit * TICKS + at, []):
                push_all(which, t)
            if at > 0:
                advance(per_tick)
            if at == 5 and unit == last:
                push(unit, 1, 0)

        compute(unit, ticks)
        if unit < last:
            while any(hop[0] <= unit + 1 for hop in pulls):
                advance(1)
            pulled(unit + 1)
    push(last, 1, 1)
    for which, t in due.get((last + 1) * TICKS, []):
        push_all(which, t)
    for t in range(2, far + 1):
        push(last, t, 0)
        push(last, t, 1)
        if closing:
            which = closing.pop(0)
            for part in parts_out(which):
                finish(which, part)
    for which in closing:
        for part in parts_out(which):
            finish(which, part)
    finish(last, 0)
    finish(last, 1)
    for copy in moved.values():
        copy.wait_send()
    for copy in sent.values():
        copy.wait_send()
    for _, away, _ in entries:
        away.wait_send()
    for copy in outgoing:
        copy.wait()


def key_block(prompt, resp):
    size = 256
    while prompt % size or resp % size:
        size //= 2
    return size


def settle_kernel(*refs):
    count = (len(refs) - 2) // 3
    sources, targets, holds = refs[:count], refs[count : 2 * count], refs[2 * count : 3 * count]
    taken, given = refs[3 * count :]
    pieces = []
    for i, (source, target, hold) in enumerate(zip(sources, targets, holds)):
        chunks = 4 if source.size > 1 << 18 else 1
        step = source.shape[-1] // chunks
        for c in range(chunks):
            cut = (slice(None),) * (len(source.shape) - 1) + (pl.ds(c * step, step),)
            taking = pltpu.make_async_copy(source.at[cut], hold.at[cut], taken.at[i, c])
            taking.start()
            giving = pltpu.make_async_copy(hold.at[cut], target.at[cut], given.at[i, c])
            pieces.append((taking, giving))
    for taking, giving in pieces:
        taking.wait()
        giving.start()
    for _, giving in pieces:
        giving.wait()


def settle(*arrays):
    hbm = pl.BlockSpec(memory_space=pl.ANY)
    dma = pltpu.SemaphoreType.DMA
    return pl.pallas_call(
        settle_kernel,
        out_shape=tuple(jax.ShapeDtypeStruct(x.shape, x.dtype) for x in arrays),
        in_specs=[hbm] * len(arrays),
        out_specs=(hbm,) * len(arrays),
        scratch_shapes=[pltpu.VMEM(x.shape, x.dtype) for x in arrays]
        + [dma((len(arrays), 4)), dma((len(arrays), 4))],
        compiler_params=pltpu.CompilerParams(vmem_limit_bytes=60 * MIB),
        name="settle",
    )(*arrays)


def local(prompt_keys, prompt_values, queries, resp_keys, resp_values, cotangent, lengths):
    devices = lax.axis_size("ctx")
    n = devices // 2
    prows, columns = prompt_keys.shape
    rows, wide = queries.shape[1], queries.shape[2] // 2
    heads = columns // 2 // HEAD_DIM
    prompt, resp = prows * devices, rows * devices
    smem = pl.BlockSpec(memory_space=pltpu.SMEM)
    hbm = pl.BlockSpec(memory_space=pl.ANY)
    shape = jax.ShapeDtypeStruct
    bf16, f32 = jnp.bfloat16, jnp.float32
    vmem, dma = pltpu.VMEM, pltpu.SemaphoreType.DMA
    hop, units = n // 2, 2 * heads
    block = key_block(prompt, resp)
    lanes = 2 * rows * (wide // HEAD_DIM) // heads
    total = prompt + resp
    gq, grk, grv, gpk, gpv = pl.pallas_call(
        functools.partial(fused_kernel, n, block),
        out_shape=(
            shape((2, rows, 2 * wide), f32),
            shape((2, rows, columns), f32), shape((2, rows, columns), f32),
            shape((prows, columns), f32), shape((prows, columns), f32),
        ),
        in_specs=[smem] + [hbm] * 6,
        out_specs=(hbm,) * 5,
        scratch_shapes=[
            vmem((2, heads, prompt, HEAD_DIM), bf16),
            vmem((2, heads, 2, resp, HEAD_DIM), bf16),
            vmem((2, 2, rows, wide), bf16), vmem((2, 2, rows, wide), bf16),
            vmem((lanes, HEAD_DIM), bf16), vmem((lanes, HEAD_DIM), bf16),
            vmem((total, lanes), f32), vmem((total, lanes), f32),
            vmem((HEAD_DIM, lanes), f32),
            vmem((1, lanes), f32), vmem((1, lanes), f32), vmem((1, lanes), f32),
            vmem((2, heads, prompt, HEAD_DIM), f32),
            vmem((2, heads, 2, resp, HEAD_DIM), f32),
            vmem((2, 2, heads, hop, 2 * prows, HEAD_DIM), bf16),
            vmem((2, 2, units, hop, 2 * rows, HEAD_DIM), bf16),
            vmem((2, 2, heads, hop, 2 * prows, HEAD_DIM), bf16),
            vmem((2, 2, units, hop, 2 * rows, HEAD_DIM), bf16),
            vmem((2, heads, 2 * prows, HEAD_DIM), f32),
            vmem((2, heads, 2, 2 * rows, HEAD_DIM), f32),
            vmem((2, 2, rows, wide), f32),
            dma((2, 2, units, 2, hop)), dma((2, 2, units, 2, hop)),
            dma((2, 2, units, 2, hop)), dma((2, 2, units, 2, hop)),
            dma((2, units, 2)), dma((2, units, 2)), dma((2, units, 2)),
            dma((2 + units,)), dma((2 + units,)), dma((2 + units,)),
            dma((2, units, 2)), dma((2, units, 2)), dma((2, units, 2)),
        ],
        compiler_params=pltpu.CompilerParams(
            collective_id=0, has_side_effects=True, vmem_limit_bytes=60 * MIB
        ),
        name="fused",
    )(lengths, prompt_keys, prompt_values, resp_keys, resp_values, queries, cotangent)
    return settle(gq, grk, grv, gpk, gpv)


def solution(mesh):
    placed = (
        P(("pairs", "ctx"), None),
        P(("pairs", "ctx"), None),
        P("pairs", "ctx", None),
        P("pairs", "ctx", None),
        P("pairs", "ctx", None),
        P("pairs", "ctx", None),
        P("pairs"),
    )
    return jax.shard_map(
        local,
        mesh=mesh,
        in_specs=placed,
        out_specs=(
            P("pairs", "ctx", None),
            P("pairs", "ctx", None),
            P("pairs", "ctx", None),
            P(("pairs", "ctx"), None),
            P(("pairs", "ctx"), None),
        ),
        check_vma=False,
    )
```

profile of v0, /device:TPU:0, one launch (start us, length us, event | category | flops | bytes accessed | tf_op | source)
XLA Modules:
  0.0 72.4 jit_solution(7606673904554135281)
XLA Ops:
  0.6 68.9 %fused.1 = (f32[2,48,4096]{2,1,0:T(8,128)}, f32[2,48,512]{2,1,0:T(8,128)}, f32[2,48,512]{2,1,0:T(8,128)}, f32[32,512]{1,0:T(8,128)}, f32[32,512]{1,0:T(8,128)}) custom-call(s32[2]{0:T(128)} %lengths.1, bf16[32,512]{1,0:T(8,128)(2,1)} %pk.1, bf16[32,512]{1,0:T(8,128)(2,1)} %pv.1, bf16[2,48,512]{2,1,0:T(8,128)(2,1)} %rk.1, bf16[2,48,512]{2,1,0:T(8,128)(2,1)} %rv.1, ...), custom_call_target="tpu_custom_call" | custom-call | tf_op jit(solution)/shard_map/fused/pallas_call | solution.py:462
  69.5 2.6 %settle.1 = (f32[2,48,4096]{2,1,0:T(8,128)}, f32[2,48,512]{2,1,0:T(8,128)}, f32[2,48,512]{2,1,0:T(8,128)}, f32[32,512]{1,0:T(8,128)}, f32[32,512]{1,0:T(8,128)}) custom-call(f32[2,48,4096]{2,1,0:T(8,128)} %get-tuple-element.10.refs_0_, f32[2,48,512]{2,1,0:T(8,128)} %get-tuple-element.11.refs_1_, f32[2,48,512]{2,1,0:T(8,128)} %get-tuple-element.12.refs_2_, ...), custom_call_target="tpu_custom_call" | custom-call | tf_op jit(solution)/shard_map/settle/pallas_call | solution.py:434
where the time goes:
time: 72.5 us; the launch traced here: 72.4 us
  Pallas kernels  71.6 us (99%)
  between operations  0.8 us (1%)
    pallas_call x1, Pallas kernels, local(): pl.pallas_call(functools.partial(fused_kernel, n, block), out_shape=(shap...  68.9 us
    pallas_call x1, Pallas kernels, settle(): pl.pallas_call(settle_kernel, out_shape=tuple((jax.ShapeDtypeStruct(x.sha...  2.65 us

commit v1 on v0

v1 whole, which is shorter than its diff:
```python
import functools

import jax
import jax.numpy as jnp
from jax import lax
from jax.experimental import pallas as pl
from jax.experimental.pallas import tpu as pltpu
from jax.sharding import PartitionSpec as P

HEAD_DIM = 128
SCALE = HEAD_DIM ** (-0.5)
LOG2E = 1.4426950408889634
MIB = 1024 * 1024
RELAYED = 3


def remote(src, dst, send, recv, device):
    return pltpu.make_async_remote_copy(
        src_ref=src,
        dst_ref=dst,
        send_sem=send,
        recv_sem=recv,
        device_id={"ctx": device},
        device_id_type=pl.DeviceIdType.MESH,
    )


def offsets(groups, signs):
    order = [3] + list(range(4, groups)) + [1, 2]
    return [sign * far for far in order if far < groups for sign in signs]


def fused_kernel(
    groups, block, lengths, pk, pv, rk, rv, q, u,
    gq, grk, grv, gpk, gpv,
    kp, kr, kpos, qh, uh, qs, us, s_buf, d_buf, qt_buf, m_buf, l_buf, e_buf,
    tp, tr, xp, xr, sp, sr, rp, rr, lp, lr, fp, fr, dq,
    ysend, yrecv, ylocal, asend, arecv, bsend, dsend, drecv,
    csend, crecv, zsend, zrecv, lrecv, fsend, frecv, flocal,
    qsend, qrecv, qlocal, gsend, grecv, glocal,
):
    me = lax.axis_index("ctx")
    core, side, group = me % 2, (me // 2) % 2, me // 4

    def device(where, y, c):
        return where * 4 + y * 2 + c

    partner = device(group, side, 1 - core)
    across = device(group, 1 - side, core)
    prows, rrows = pk.shape[0], rk.shape[1]
    heads = kp.shape[1]
    wide = q.shape[2] // 2
    span = wide // heads
    members = span // HEAD_DIM
    inputs = ((pk, rk), (pv, rv))
    outputs = ((gpk, grk), (gpv, grv))
    parts = (0, 1, 2)
    pending = []

    def size_of(part):
        return prows if part == 0 else rrows

    def signs_out(part):
        return (1, -1) if part == 0 else (1,)

    def signs_back(part):
        return (-1, 1) if part == 0 else (-1,)

    def at_row(start, size):
        return pl.ds(pl.multiple_of(start, 16), size)

    def block_rows(part, c, where):
        size = 2 * size_of(part)
        return at_row(c * groups * size + where * size, size)

    def half_rows(part, where):
        size = 2 * size_of(part)
        return at_row(where * size, size)

    def own_rows(part):
        size = size_of(part)
        return at_row(core * groups * 2 * size + group * 2 * size + side * size, size)

    def pick(pair, k, part):
        return pair[0].at[:, k] if part == 0 else pair[1].at[:, k, part - 1]

    def stack(pair, k, part):
        return pair[0].at[k] if part == 0 else pair[1].at[k, part - 1]

    def head_columns(y, k):
        return pl.ds(pl.multiple_of((y * heads + k) * HEAD_DIM, HEAD_DIM), HEAD_DIM)

    def given(kind, part, cols):
        ref = inputs[kind][min(part, 1)]
        return ref.at[:, cols] if part == 0 else ref.at[part - 1, :, cols]

    def valid(where):
        return jnp.logical_and(where >= 0, where < groups)

    def later(cond, copy):
        pending.append((cond, copy))

    units = [(k, b) for k in range(heads) for b in range(2)]
    order = [(k, part) for k in range(heads) for part in parts]

    stays = {}
    for k, part in order:
        for kind in range(2):
            dst = pick((kp, kr), k, part).at[kind, own_rows(part), :]
            stay = pltpu.make_async_copy(
                given(kind, part, head_columns(side, k)), dst, ylocal.at[part, k, kind]
            )
            stay.start()
            stays[k, part, kind] = stay
    query_stays = {}
    for k, b in units:
        cols = pl.ds(pl.multiple_of((side * heads + k) * span, span), span)
        for i, (src, dst) in enumerate(((q, qh), (u, uh))):
            stay = pltpu.make_async_copy(
                src.at[b, :, cols], dst.at[side, b, :, pl.ds(k * span, span)], qlocal.at[i, k, b]
            )
            stay.start()
            query_stays[i, k, b] = stay

    for c in range(2):
        for where in range(groups):
            @pl.when(where > group)
            def _(c=c, where=where):
                empty = jnp.zeros((2, heads, 2, 2 * rrows, HEAD_DIM), kr.dtype)
                kr[:, :, :, pl.ds((c * groups + where) * 2 * rrows, 2 * rrows), :] = empty
            for y in range(2):
                start = ((c * groups + where) * 2 + y) * rrows
                kpos[pl.ds(start, rrows), :] = device(where, y, c) * rrows + lax.broadcasted_iota(
                    jnp.int32, (rrows, 1), 0
                )
    for ref in (rp, rr, lp, lr):
        ref[...] = jnp.zeros_like(ref)

    barrier = pltpu.get_barrier_semaphore()
    peers = [partner, across] + [device((group + i) % groups, side, core) for i in range(1, groups)]
    for other in peers:
        pl.semaphore_signal(
            barrier, inc=1, device_id={"ctx": other}, device_id_type=pl.DeviceIdType.MESH
        )
    pl.semaphore_wait(barrier, len(peers))

    crossing = {}
    for k, part in order:
        for kind in range(2):
            dst = pick((kp, kr), k, part).at[kind, own_rows(part), :]
            away = remote(
                given(kind, part, head_columns(1 - side, k)), dst,
                ysend.at[part, k, kind], yrecv.at[part, k, kind], across,
            )
            away.start()
            crossing[k, part, kind] = away
            later(None, away)
    query_moves = {}
    for k, b in units:
        cols = pl.ds(pl.multiple_of(((1 - side) * heads + k) * span, span), span)
        for i, (src, dst) in enumerate(((q, qh), (u, uh))):
            away = remote(
                src.at[b, :, cols], dst.at[side, b, :, pl.ds(k * span, span)],
                qsend.at[i, k, b], qrecv.at[i, k, b], across,
            )
            away.start()
            query_moves[i, k, b] = away
            later(None, away)

    def shared(k, part, where):
        ref = pick((kp, kr), k, part).at[:, block_rows(part, core, where), :]
        return remote(ref, ref, dsend.at[part, k, where], drecv.at[part, k, where], partner)

    def fan(k, part):
        for kind in range(2):
            crossing[k, part, kind].wait_recv()
            stays[k, part, kind].wait()
        ref = pick((kp, kr), k, part).at[:, block_rows(part, core, group), :]
        near = shared(k, part, group)
        near.start()
        later(None, near)
        for i, delta in enumerate(offsets(groups, signs_out(part))):
            if abs(delta) == RELAYED:
                continue
            to = group + delta
            copy = remote(
                ref, ref, asend.at[part, k, i], arecv.at[part, k, group], device(to, side, core)
            )
            pl.when(valid(to))(copy.start)
            later(valid(to), copy)

    def arrive(k, part, delta):
        origin = group - delta
        step = 1 if delta > 0 else -1
        ref = pick((kp, kr), k, part).at[:, block_rows(part, core, origin), :]
        copy = remote(ref, ref, asend.at[part, k, 0], arecv.at[part, k, origin], partner)
        near = shared(k, part, origin)

        @pl.when(valid(origin))
        def _():
            copy.wait_recv()
            near.start()

        later(valid(origin), near)
        if abs(delta) == RELAYED - 1:
            go = jnp.logical_and(valid(origin), valid(group + step))
            copy = remote(
                ref, ref, bsend.at[part, k, 0 if step > 0 else 1], arecv.at[part, k, origin],
                device(group + step, side, core),
            )
            pl.when(go)(copy.start)
            later(go, copy)

    def arrivals(k, part):
        near_first = sorted(offsets(groups, signs_out(part)), key=abs)
        return [(k, part, delta) for delta in near_first]

    def gathered(k, part):
        shared(k, part, group).wait_recv()
        for delta in offsets(groups, signs_out(part)):
            origin = group - delta
            pl.when(valid(origin))(shared(k, part, origin).wait_recv)

    def meet(k, part):
        rows = block_rows(part, 1 - core, 0)
        size = groups * 2 * size_of(part)
        rows = at_row((1 - core) * size, size)
        copy = remote(
            pick((tp, tr), k, part).at[:, rows, :], pick((xp, xr), k, part),
            csend.at[part, k], crecv.at[part, k], partner,
        )
        copy.start()
        later(None, copy)
        met[k, part] = copy

    met = {}

    def total(kind, k, part, where):
        mine = pick((tp, tr), k, part).at[kind, block_rows(part, core, where), :]
        other = pick((xp, xr), k, part).at[kind, half_rows(part, where), :]
        return mine[...] + other[...]

    def push(k, part, fars):
        signs = signs_back(part)
        for i, delta in enumerate(offsets(groups, signs)):
            if abs(delta) not in fars:
                continue
            step = 1 if delta > 0 else -1
            way = 0 if step < 0 else 1
            to = group + delta
            out = stack((sp, sr), k, part).at[i]
            passing = stack((lp, lr), k, part).at[way]
            relayed = abs(delta) == RELAYED
            gathers = abs(delta) == RELAYED - 1
            if relayed:
                dst, recv, where = passing, lrecv.at[part, k, way], group + step
            else:
                dst = stack((rp, rr), k, part).at[group]
                recv, where = zrecv.at[part, k, group], to
            copy = remote(out, dst, zsend.at[part, k, i], recv, device(where, side, core))
            if gathers:
                wait = remote(out, passing, zsend.at[part, k, i], lrecv.at[part, k, way], partner)
                pl.when(jnp.logical_and(valid(to), valid(group - step)))(wait.wait_recv)

            @pl.when(valid(to))
            def _(delta=delta, to=to, out=out, passing=passing, gathers=gathers, copy=copy):
                for kind in range(2):
                    value = total(kind, k, part, to)
                    if gathers:
                        value = value + passing[kind].astype(jnp.float32)
                    out[kind] = value.astype(jnp.bfloat16)
                copy.start()

            later(valid(to), copy)

    def finish(k, part):
        got = stack((rp, rr), k, part)
        final = stack((fp, fr), k, part)
        for delta in offsets(groups, signs_back(part)):
            if abs(delta) == RELAYED:
                continue
            origin = group - delta
            slot = got.at[origin]
            copy = remote(slot, slot, zsend.at[part, k, 0], zrecv.at[part, k, origin], partner)
            pl.when(valid(origin))(copy.wait_recv)
        for kind in range(2):
            value = total(kind, k, part, group)
            for origin in range(groups):
                value = value + got[origin, kind].astype(jnp.float32)
            final[kind] = value.astype(jnp.bfloat16)
            out = outputs[kind][min(part, 1)]
            cols = head_columns(side, k)
            dst = out.at[:, cols] if part == 0 else out.at[part - 1, :, cols]
            size = size_of(part)
            away = remote(
                final.at[kind, at_row((1 - side) * size, size), :], dst,
                fsend.at[part, k, kind], frecv.at[part, k, kind], across,
            )
            away.start()
            stay = pltpu.make_async_copy(
                final.at[kind, at_row(side * size, size), :], dst, flocal.at[part, k, kind]
            )
            stay.start()
            outgoing.extend((away, stay))

    outgoing = []
    half = members * rrows
    lanes = 2 * half
    prompt_blocks = kp.shape[2] // block
    resp_blocks = kr.shape[3] // block
    factor = SCALE * LOG2E
    lane = lax.broadcasted_iota(jnp.int32, (1, lanes), 1)
    row_of = lax.rem(lane, rrows)
    first_row = device(group, 0, core) * rrows
    positions = first_row + row_of + jnp.where(lane < half, 0, 2 * rrows)
    row_iota = lax.broadcasted_iota(jnp.int32, (rrows, 1), 0)
    nt = (((1,), (1,)), ((), ()))

    def key_rows(j):
        return pl.ds(pl.multiple_of(j * block, block), block)

    def compute(unit, ticks):
        k, b = units[unit]
        length = lengths[b]
        for source in range(2):
            live = first_row + source * 2 * rrows + row_iota < length
            for g in range(members):
                cols = pl.ds((k * members + g) * HEAD_DIM, HEAD_DIM)
                at = pl.ds(source * half + g * rrows, rrows)
                qs[at, :] = qh[source, b, :, cols]
                rows = uh[source, b, :, cols]
                us[at, :] = jnp.where(live, rows, jnp.zeros_like(rows))
        m_buf[...] = jnp.full_like(m_buf, -jnp.inf)
        l_buf[...] = jnp.zeros_like(l_buf)
        e_buf[...] = jnp.zeros_like(e_buf)
        qt_buf[...] = jnp.zeros_like(qt_buf)
        ticks(0)

        def scores(keys, at, j, causal):
            s = lax.dot_general(keys, qs[...], nt, preferred_element_type=jnp.float32)
            if causal:
                s = jnp.where(kpos[key_rows(j), :] <= positions, s, -jnp.inf)
            s_buf[at, :] = s
            m_buf[...] = jnp.maximum(m_buf[...], jnp.max(s, axis=0, keepdims=True))

        @pl.loop(0, prompt_blocks, unroll=True)
        def _(j):
            scores(kp[0, k, key_rows(j), :], key_rows(j), j, False)

        ticks(1)

        @pl.loop(0, resp_blocks, unroll=True)
        def _(j):
            scores(kr[0, k, b, key_rows(j), :], key_rows(prompt_blocks + j), j, True)

        ticks(2)
        shift = m_buf[...] * factor

        def weights(vals, at):
            p = jnp.exp2(s_buf[at, :] * factor - shift)
            d = lax.dot_general(vals, us[...], nt, preferred_element_type=jnp.float32)
            l_buf[...] += jnp.sum(p, axis=0, keepdims=True)
            e_buf[...] += jnp.sum(p * d, axis=0, keepdims=True)
            s_buf[at, :] = p
            d_buf[at, :] = d

        @pl.loop(0, prompt_blocks, unroll=True)
        def _(j):
            weights(kp[1, k, key_rows(j), :], key_rows(j))

        ticks(3)

        @pl.loop(0, resp_blocks, unroll=True)
        def _(j):
            weights(kr[1, k, b, key_rows(j), :], key_rows(prompt_blocks + j))

        ticks(4)
        inverse = 1.0 / l_buf[...]
        delta = e_buf[...] * inverse

        def grads(keys, at):
            p = s_buf[at, :] * inverse
            ds = (p * (d_buf[at, :] - delta)).astype(jnp.bfloat16)
            dv = jnp.dot(p.astype(jnp.bfloat16), us[...], preferred_element_type=jnp.float32)
            dk = jnp.dot(ds, qs[...], preferred_element_type=jnp.float32) * SCALE
            qt_buf[...] += jnp.dot(keys.T, ds, preferred_element_type=jnp.float32)
            return dk, dv

        @pl.loop(0, prompt_blocks, unroll=True)
        def _(j):
            at = key_rows(j)
            pair = grads(kp[0, k, at, :], at)
            for kind in range(2):
                if b == 0:
                    tp[kind, k, at, :] = pair[kind]
                else:
                    tp[kind, k, at, :] += pair[kind]

        ticks(5)

        @pl.loop(0, resp_blocks, unroll=True)
        def _(j):
            at = key_rows(j)
            pair = grads(kr[0, k, b, at, :], key_rows(prompt_blocks + j))
            for kind in range(2):
                tr[kind, k, b, at, :] = pair[kind]

        ticks(6)
        result = (qt_buf[...].T * SCALE).astype(jnp.bfloat16)
        for source in range(2):
            for g in range(members):
                start = source * half + g * rrows
                dq[source, b, :, pl.ds((k * members + g) * HEAD_DIM, HEAD_DIM)] = result[
                    start : start + rrows
                ]
        cols = pl.ds(k * span, span)
        to = pl.ds(pl.multiple_of((side * heads + k) * span, span), span)
        away = remote(
            dq.at[1 - side, b, :, cols], gq.at[b, :, to], gsend.at[k, b], grecv.at[k, b], across
        )
        away.start()
        stay = pltpu.make_async_copy(dq.at[side, b, :, cols], gq.at[b, :, to], glocal.at[k, b])
        stay.start()
        outgoing.extend((away, stay))

    def needs(unit):
        k, b = units[unit]
        return [(k, 0), (k, 1)] if b == 0 else [(k, 2)]

    def yields(unit):
        k, b = units[unit]
        return [(k, 1)] if b == 0 else [(k, 0), (k, 2)]

    fars = sorted({abs(delta) for delta in offsets(groups, (1,))})
    early = tuple(far for far in fars if far != RELAYED - 1)
    late = tuple(far for far in fars if far == RELAYED - 1)

    for k, part in order:
        fan(k, part)
    for k, part in needs(0):
        for item in arrivals(k, part):
            arrive(*item)
    for k, part in needs(0):
        gathered(k, part)

    last = len(units) - 1
    for unit in range(last + 1):
        k, b = units[unit]
        for i in range(2):
            query_stays[i, k, b].wait()
            query_moves[i, k, b].wait_recv()

        def ticks(at, unit=unit, k=k, b=b):
            if unit < last:
                if at == 4:
                    for pair in needs(unit + 1):
                        for item in arrivals(*pair):
                            arrive(*item)
            if unit > 0:
                if at == 1:
                    for pair in yields(unit - 1):
                        met[pair].wait_recv()
                        push(*pair, early)
                if at == 3:
                    for pair in yields(unit - 1):
                        push(*pair, late)
            if unit > 1 and at == 2:
                for pair in yields(unit - 2):
                    finish(*pair)
            if at == 5 and b == 1:
                meet(k, 0)
            if at == 6:
                meet(k, b + 1)

        compute(unit, ticks)
        if unit < last:
            for pair in needs(unit + 1):
                gathered(*pair)
    for pair in yields(last):
        met[pair].wait_recv()
        push(*pair, early)
    for pair in yields(last):
        push(*pair, late)
    for pair in yields(last - 1) + yields(last):
        finish(*pair)
    for cond, copy in pending:
        if cond is None:
            copy.wait_send()
        else:
            pl.when(cond)(copy.wait_send)
    for copy in outgoing:
        copy.wait()


def key_block(prompt, resp):
    size = 256
    while prompt % size or resp % size:
        size //= 2
    return size


def settle_kernel(*refs):
    count = (len(refs) - 2) // 4
    sources, targets = refs[:count], refs[count : 2 * count]
    holds, wides = refs[2 * count : 3 * count], refs[3 * count : 4 * count]
    taken, given = refs[4 * count :]
    pieces = []
    for i, (source, target, hold, wide) in enumerate(zip(sources, targets, holds, wides)):
        chunks = 4 if source.size > 1 << 18 else 1
        step = source.shape[-1] // chunks
        for c in range(chunks):
            cut = (slice(None),) * (len(source.shape) - 1) + (pl.ds(c * step, step),)
            taking = pltpu.make_async_copy(source.at[cut], hold.at[cut], taken.at[i, c])
            taking.start()
            giving = pltpu.make_async_copy(wide.at[cut], target.at[cut], given.at[i, c])
            pieces.append((taking, giving, hold, wide, cut))
    for taking, giving, hold, wide, cut in pieces:
        taking.wait()
        wide[cut] = hold[cut].astype(wide.dtype)
        giving.start()
    for piece in pieces:
        piece[1].wait()


def settle(*arrays):
    hbm = pl.BlockSpec(memory_space=pl.ANY)
    dma = pltpu.SemaphoreType.DMA
    return pl.pallas_call(
        settle_kernel,
        out_shape=tuple(jax.ShapeDtypeStruct(x.shape, jnp.float32) for x in arrays),
        in_specs=[hbm] * len(arrays),
        out_specs=(hbm,) * len(arrays),
        scratch_shapes=[pltpu.VMEM(x.shape, x.dtype) for x in arrays]
        + [pltpu.VMEM(x.shape, jnp.float32) for x in arrays]
        + [dma((len(arrays), 4)), dma((len(arrays), 4))],
        compiler_params=pltpu.CompilerParams(vmem_limit_bytes=60 * MIB),
        name="settle",
    )(*arrays)


def local(prompt_keys, prompt_values, queries, resp_keys, resp_values, cotangent, lengths):
    devices = lax.axis_size("ctx")
    groups = devices // 4
    prows, columns = prompt_keys.shape
    rows, wide = queries.shape[1], queries.shape[2] // 2
    heads = columns // 2 // HEAD_DIM
    prompt, resp = prows * devices, rows * devices
    smem = pl.BlockSpec(memory_space=pltpu.SMEM)
    hbm = pl.BlockSpec(memory_space=pl.ANY)
    shape = jax.ShapeDtypeStruct
    bf16, f32 = jnp.bfloat16, jnp.float32
    vmem, dma = pltpu.VMEM, pltpu.SemaphoreType.DMA
    block = key_block(prompt, resp)
    lanes = 2 * rows * (wide // HEAD_DIM) // heads
    total = prompt + resp
    both, one = len(offsets(groups, (1, -1))), len(offsets(groups, (1,)))
    outs = pl.pallas_call(
        functools.partial(fused_kernel, groups, block),
        out_shape=(
            shape((2, rows, 2 * wide), bf16),
            shape((2, rows, columns), bf16), shape((2, rows, columns), bf16),
            shape((prows, columns), bf16), shape((prows, columns), bf16),
        ),
        in_specs=[smem] + [hbm] * 6,
        out_specs=(hbm,) * 5,
        scratch_shapes=[
            vmem((2, heads, prompt, HEAD_DIM), bf16),
            vmem((2, heads, 2, resp, HEAD_DIM), bf16),
            vmem((resp, 1), jnp.int32),
            vmem((2, 2, rows, wide), bf16), vmem((2, 2, rows, wide), bf16),
            vmem((lanes, HEAD_DIM), bf16), vmem((lanes, HEAD_DIM), bf16),
            vmem((total, lanes), f32), vmem((total, lanes), f32),
            vmem((HEAD_DIM, lanes), f32),
            vmem((1, lanes), f32), vmem((1, lanes), f32), vmem((1, lanes), f32),
            vmem((2, heads, prompt, HEAD_DIM), f32),
            vmem((2, heads, 2, resp, HEAD_DIM), f32),
            vmem((2, heads, prompt // 2, HEAD_DIM), f32),
            vmem((2, heads, 2, resp // 2, HEAD_DIM), f32),
            vmem((heads, both, 2, 2 * prows, HEAD_DIM), bf16),
            vmem((heads, 2, one, 2, 2 * rows, HEAD_DIM), bf16),
            vmem((heads, groups, 2, 2 * prows, HEAD_DIM), bf16),
            vmem((heads, 2, groups, 2, 2 * rows, HEAD_DIM), bf16),
            vmem((heads, 2, 2, 2 * prows, HEAD_DIM), bf16),
            vmem((heads, 2, 1, 2, 2 * rows, HEAD_DIM), bf16),
            vmem((heads, 2, 2 * prows, HEAD_DIM), bf16),
            vmem((heads, 2, 2, 2 * rows, HEAD_DIM), bf16),
            vmem((2, 2, rows, wide), bf16),
            dma((3, heads, 2)), dma((3, heads, 2)), dma((3, heads, 2)),
            dma((3, heads, both)), dma((3, heads, groups)), dma((3, heads, 2)),
            dma((3, heads, groups)), dma((3, heads, groups)),
            dma((3, heads)), dma((3, heads)),
            dma((3, heads, both)), dma((3, heads, groups)), dma((3, heads, 2)),
            dma((3, heads, 2)), dma((3, heads, 2)), dma((3, heads, 2)),
            dma((2, heads, 2)), dma((2, heads, 2)), dma((2, heads, 2)),
            dma((heads, 2)), dma((heads, 2)), dma((heads, 2)),
        ],
        compiler_params=pltpu.CompilerParams(
            collective_id=0, has_side_effects=True, vmem_limit_bytes=60 * MIB
        ),
        name="fused",
    )(lengths, prompt_keys, prompt_values, resp_keys, resp_values, queries, cotangent)
    return settle(*outs)


def solution(mesh):
    placed = (
        P(("pairs", "ctx"), None),
        P(("pairs", "ctx"), None),
        P("pairs", "ctx", None),
        P("pairs", "ctx", None),
        P("pairs", "ctx", None),
        P("pairs", "ctx", None),
        P("pairs"),
    )
    return jax.shard_map(
        local,
        mesh=mesh,
        in_specs=placed,
        out_specs=(
            P("pairs", "ctx", None),
            P("pairs", "ctx", None),
            P("pairs", "ctx", None),
            P(("pairs", "ctx"), None),
            P(("pairs", "ctx"), None),
        ),
        check_vma=False,
    )
```

time: 72.5 us -> 71.3 us (0.983)
  Pallas kernels: 71.6 us -> 70.4 us
    pallas_call x1, Pallas kernels: 68.9 us -> 67.8 us  [local(): pl.pallas_call(functools.partial(fused_kernel, groups, block), out_shape=...]
where the time goes in v1:
time: 71.3 us; the launch traced here: 71.2 us
  Pallas kernels  70.4 us (99%)
  between operations  0.8 us (1%)
    pallas_call x1, Pallas kernels, local(): pl.pallas_call(functools.partial(fused_kernel, groups, block), out_shape=...  67.8 us
    pallas_call x1, Pallas kernels, settle(): pl.pallas_call(settle_kernel, out_shape=tuple((jax.ShapeDtypeStruct(x.sha...  2.61 us

profile of v1, /device:TPU:0, one launch (start us, length us, event | category | flops | bytes accessed | tf_op | source)
XLA Modules:
  0.0 71.2 jit_solution(8549056206381773530)
XLA Ops:
  0.6 67.8 %fused.1 = (bf16[2,48,4096]{2,1,0:T(8,128)(2,1)}, bf16[2,48,512]{2,1,0:T(8,128)(2,1)}, bf16[2,48,512]{2,1,0:T(8,128)(2,1)}, bf16[32,512]{1,0:T(8,128)(2,1)}, bf16[32,512]{1,0:T(8,128)(2,1)}) custom-call(s32[2]{0:T(128)} %lengths.1, bf16[32,512]{1,0:T(8,128)(2,1)} %pk.1, bf16[32,512]{1,0:T(8,128)(2,1)} %pv.1, bf16[2,48,512]{2,1,0:T(8,128)(2,1)} %rk.1, ...), custom_call_target="tpu_custom_call" | custom-call | tf_op jit(solution)/shard_map/fused/pallas_call | solution.py:557
  68.4 2.6 %settle.1 = (f32[2,48,4096]{2,1,0:T(8,128)}, f32[2,48,512]{2,1,0:T(8,128)}, f32[2,48,512]{2,1,0:T(8,128)}, f32[32,512]{1,0:T(8,128)}, f32[32,512]{1,0:T(8,128)}) custom-call(bf16[2,48,4096]{2,1,0:T(8,128)(2,1)} %get-tuple-element.10.refs_0_, bf16[2,48,512]{2,1,0:T(8,128)(2,1)} %get-tuple-element.11.refs_1_, bf16[2,48,512]{2,1,0:T(8,128)(2,1)} %get-tuple-element.12.refs_2_, ...), custom_call_target="tpu_custom_call" | custom-call | tf_op jit(solution)/shard_map/settle/pallas_call | solution.py:528

commit v2 on v1

v2 whole, which is shorter than its diff:
```python
import functools

import jax
import jax.numpy as jnp
from jax import lax
from jax.experimental import pallas as pl
from jax.experimental.pallas import tpu as pltpu
from jax.sharding import PartitionSpec as P

HEAD_DIM = 128
SCALE = HEAD_DIM ** (-0.5)
LOG2E = 1.4426950408889634
MIB = 1024 * 1024
RELAYED = 3


def remote(src, dst, send, recv, device):
    return pltpu.make_async_remote_copy(
        src_ref=src,
        dst_ref=dst,
        send_sem=send,
        recv_sem=recv,
        device_id={"ctx": device},
        device_id_type=pl.DeviceIdType.MESH,
    )


def offsets(groups, signs):
    order = [2, 1, 3] + list(range(4, groups))
    return [sign * far for far in order if far < groups for sign in signs]


def fused_kernel(
    groups, block, lengths, pk, pv, rk, rv, q, u,
    gq, grk, grv, gpk, gpv,
    kp, kr, bp, br, kpos, quh, quf, qs, us, s_buf, d_buf, qt_buf, m_buf, l_buf, e_buf,
    tp, tr, xp, xr, sp, sr, rp, rr, fb, dq,
    local_sem, ysend, yrecv, qsend, qrecv, asend_p, asend_r, arecv, bsend, dsend, drecv,
    csend, crecv, zsend_p, zsend_r, zrecv, fsem, gsem,
):
    me = lax.axis_index("ctx")
    core, side, group = me % 2, (me // 2) % 2, me // 4

    def device(where, y, c):
        return where * 4 + y * 2 + c

    partner = device(group, side, 1 - core)
    across = device(group, 1 - side, core)
    prows, rrows = pk.shape[0], rk.shape[1]
    heads = kp.shape[1]
    wide = q.shape[2] // 2
    span = wide // heads
    members = span // HEAD_DIM
    inputs = ((pk, rk), (pv, rv))
    outputs = ((gpk, grk), (gpv, grv))
    parts = (0, 1, 2)

    def size_of(part):
        return prows if part == 0 else rrows

    def signs_out(part):
        return (1, -1) if part == 0 else (1,)

    def signs_back(part):
        return (-1, 1) if part == 0 else (-1,)

    def at_row(start, size):
        return pl.ds(pl.multiple_of(start, 16), size)

    def block_rows(part, c, where):
        size = 2 * size_of(part)
        return at_row(c * groups * size + where * size, size)

    def side_rows(part, y):
        size = size_of(part)
        return at_row(core * groups * 2 * size + group * 2 * size + y * size, size)

    def half_rows(part, where):
        size = 2 * size_of(part)
        return at_row(where * size, size)

    def core_rows(part, c):
        size = groups * 2 * size_of(part)
        return at_row(c * size, size)

    def pick(pair, k, part):
        return pair[0].at[:, k] if part == 0 else pair[1].at[:, k, part - 1]

    def stack(pair, k, part):
        return pair[0].at[k] if part == 0 else pair[1].at[k, part - 1]

    def head_columns(y, k):
        return pl.ds(pl.multiple_of((y * heads + k) * HEAD_DIM, HEAD_DIM), HEAD_DIM)

    def query_columns(y, k):
        return pl.ds(pl.multiple_of((y * heads + k) * span, span), span)

    def given(kind, part, cols):
        ref = inputs[kind][min(part, 1)]
        return ref.at[:, cols] if part == 0 else ref.at[part - 1, :, cols]

    def valid(where):
        return jnp.logical_and(where >= 0, where < groups)

    def relays(k, delta):
        return k == 0 and abs(delta) == RELAYED

    units = [(k, b) for k in range(heads) for b in range(2)]
    order = [(k, part) for k in range(heads) for part in parts]

    for c in range(2):
        for where in range(groups):
            @pl.when(where > group)
            def _(c=c, where=where):
                empty = jnp.zeros((2, heads, 2, 2 * rrows, HEAD_DIM), kr.dtype)
                kr[:, :, :, pl.ds((c * groups + where) * 2 * rrows, 2 * rrows), :] = empty
    for ref in (rp, rr):
        ref[...] = jnp.zeros_like(ref)

    barrier = pltpu.get_barrier_semaphore()
    peers = [partner, across] + [device((group + i) % groups, side, core) for i in range(1, groups)]
    for other in peers:
        pl.semaphore_signal(
            barrier, inc=1, device_id={"ctx": other}, device_id_type=pl.DeviceIdType.MESH
        )

    for k, part in order:
        for kind in range(2):
            pltpu.make_async_copy(
                given(kind, part, head_columns(1 - side, k)),
                stack((bp, br), k, part).at[kind], local_sem.at[min(part, 1)],
            ).start()
            pltpu.make_async_copy(
                given(kind, part, head_columns(side, k)),
                pick((kp, kr), k, part).at[kind, side_rows(part, side), :],
                local_sem.at[2 + min(part, 1)],
            ).start()
    wide_own = pl.ds(pl.multiple_of(side * wide, wide), wide)
    wide_far = pl.ds(pl.multiple_of((1 - side) * wide, wide), wide)
    for i, src in enumerate((q, u)):
        pltpu.make_async_copy(src.at[:, :, wide_far], quf.at[i], local_sem.at[4]).start()
        pltpu.make_async_copy(src.at[:, :, wide_own], quh.at[i, side], local_sem.at[5]).start()

    for c in range(2):
        for where in range(groups):
            for y in range(2):
                start = ((c * groups + where) * 2 + y) * rrows
                kpos[pl.ds(start, rrows), :] = device(where, y, c) * rrows + lax.broadcasted_iota(
                    jnp.int32, (rrows, 1), 0
                )

    def landed(ref, i):
        pltpu.make_async_copy(ref, ref, local_sem.at[i]).wait()

    def hello():
        pl.semaphore_wait(barrier, len(peers))

    hello()
    landed(bp, 0)
    landed(br, 1)

    def crossing(k, part, y):
        ref = pick((kp, kr), k, part).at[:, side_rows(part, y), :]
        return remote(ref, ref, ysend.at[min(part, 1)], yrecv.at[part, k], across)

    def cross(k, part):
        for kind in range(2):
            remote(
                stack((bp, br), k, part).at[kind],
                pick((kp, kr), k, part).at[kind, side_rows(part, side), :],
                ysend.at[min(part, 1)], yrecv.at[part, k], across,
            ).start()

    def query_crossing(k, b, y):
        ref = quh.at[:, y, b, :, pl.ds(k * span, span)]
        return remote(ref, ref, qsend.at[0], qrecv.at[k, b], across)

    def query_cross(k, b):
        cols = pl.ds(k * span, span)
        for i in range(2):
            remote(
                quf.at[i, b, :, cols], quh.at[i, side, b, :, cols],
                qsend.at[0], qrecv.at[k, b], across,
            ).start()

    def shared(k, part):
        ref = pick((kp, kr), k, part).at[:, core_rows(part, core), :]
        return remote(ref, ref, dsend.at[min(part, 1)], drecv.at[part, k], partner)

    def fanned(k, part, i):
        return asend_p.at[k, i] if part == 0 else asend_r.at[k, i]

    def fan(k, part):
        crossing(k, part, 1 - side).wait_recv()
        ref = pick((kp, kr), k, part).at[:, block_rows(part, core, group), :]
        for i, delta in enumerate(offsets(groups, signs_out(part))):
            if relays(k, delta):
                continue
            to = group + delta
            copy = remote(
                ref, ref, fanned(k, part, i), arecv.at[part, k, group], device(to, side, core)
            )
            pl.when(valid(to))(copy.start)

    def arrive(k, part):
        for delta in sorted(offsets(groups, signs_out(part)), key=abs):
            origin = group - delta
            step = 1 if delta > 0 else -1
            ref = pick((kp, kr), k, part).at[:, block_rows(part, core, origin), :]
            copy = remote(ref, ref, bsend.at[0], arecv.at[part, k, origin], partner)
            pl.when(valid(origin))(copy.wait_recv)
            if k == 0 and abs(delta) == RELAYED - 1:
                copy = remote(
                    ref, ref, bsend.at[2 if part > 0 else (1 - step) // 2],
                    arecv.at[part, k, origin], device(group + step, side, core),
                )
                pl.when(jnp.logical_and(valid(origin), valid(group + step)))(copy.start)
        shared(k, part).start()

    def met(k, part):
        ref = pick((tp, tr), k, part).at[:, core_rows(part, 1 - core), :]
        return remote(
            ref, pick((xp, xr), k, part), csend.at[min(part, 1)], crecv.at[part, k], partner
        )

    def meet(k, part):
        met(k, part).start()

    def total(kind, k, part, where):
        mine = pick((tp, tr), k, part).at[kind, block_rows(part, core, where), :]
        other = pick((xp, xr), k, part).at[kind, half_rows(part, where), :]
        return mine[...] + other[...]

    def returns(part):
        return offsets(groups, signs_back(part)) + [0]

    def returned(part, i):
        return zsend_p.at[i] if part == 0 else zsend_r.at[i]

    def push(k, part):
        met(k, part).wait_recv()
        size = size_of(part)
        for i, delta in enumerate(returns(part)):
            to = group + delta
            out = stack((sp, sr), k, part).at[i]
            sides = range(2) if delta else (1 - side,)
            copies = [
                remote(
                    out.at[y], stack((rp, rr), k, part).at[side, group], returned(part, i),
                    zrecv.at[part, k, group], device(to, y, core),
                )
                for y in sides
            ]

            @pl.when(valid(to))
            def _(to=to, out=out, copies=copies):
                for kind in range(2):
                    value = total(kind, k, part, to).astype(jnp.bfloat16)
                    for y in range(2):
                        out[y, kind] = value[y * size : (y + 1) * size]
                for copy in copies:
                    copy.start()

    starts = (0, prows, prows + rrows)

    def finish(k, part):
        got = stack((rp, rr), k, part)
        size = size_of(part)
        for delta in returns(part):
            origin = group - delta
            slot = got.at[:, origin] if delta else got.at[0, origin]
            copy = remote(slot, slot, bsend.at[0], zrecv.at[part, k, origin], partner)
            pl.when(valid(origin))(copy.wait_recv)
        rows = pl.ds(starts[part], size)
        near = at_row(group * 2 * size + side * size, size)
        for kind in range(2):
            mine = pick((tp, tr), k, part).at[kind, side_rows(part, side), :]
            own = mine[...] + pick((xp, xr), k, part).at[kind, near, :][...]
            out = outputs[kind][min(part, 1)]
            for y in range(2):
                value = jnp.where(side == y, own, jnp.zeros_like(own))
                for origin in range(groups):
                    value = value + got[y, origin, kind].astype(jnp.float32)
                fb[k, kind, y, rows, :] = value
                cols = pl.ds((y * heads + k) * HEAD_DIM, HEAD_DIM)
                dst = out.at[:, cols] if part == 0 else out.at[part - 1, :, cols]
                pltpu.make_async_copy(fb.at[k, kind, y, rows, :], dst, fsem.at[0]).start()

    def drain():
        remote(bp, bp, ysend.at[0], ysend.at[0], across).wait_send()
        remote(br, br, ysend.at[1], ysend.at[1], across).wait_send()
        remote(quf, quf, qsend.at[0], qsend.at[0], across).wait_send()
        ref = kp.at[:, :, core_rows(0, core), :]
        remote(ref, ref, dsend.at[0], dsend.at[0], partner).wait_send()
        ref = kr.at[:, :, :, core_rows(1, core), :]
        remote(ref, ref, dsend.at[1], dsend.at[1], partner).wait_send()
        ref = tp.at[:, :, core_rows(0, 1 - core), :]
        remote(ref, ref, csend.at[0], csend.at[0], partner).wait_send()
        ref = tr.at[:, :, :, core_rows(1, 1 - core), :]
        remote(ref, ref, csend.at[1], csend.at[1], partner).wait_send()
        for part in range(2):
            for i, delta in enumerate(offsets(groups, signs_out(part))):
                refs = []
                for k in range(heads):
                    if not relays(k, delta):
                        if part == 0:
                            ref = kp.at[:, k, block_rows(0, core, group), :]
                        else:
                            ref = kr.at[:, k, :, block_rows(1, core, group), :]
                        refs.append((ref, fanned(k, part, i)))

                @pl.when(valid(group + delta))
                def _(refs=refs):
                    for ref, sem in refs:
                        remote(ref, ref, sem, sem, across).wait_send()

                if abs(delta) == RELAYED - 1:
                    step = 1 if delta > 0 else -1
                    origin = group - delta
                    if part == 0:
                        ref = kp.at[:, 0, block_rows(0, core, origin), :]
                    else:
                        ref = kr.at[:, 0, :, block_rows(1, core, origin), :]
                    sem = bsend.at[2 if part > 0 else (1 - step) // 2]
                    pl.when(jnp.logical_and(valid(origin), valid(group + step)))(
                        remote(ref, ref, sem, sem, across).wait_send
                    )
            for i, delta in enumerate(returns(part)):
                ref = sp.at[:, i] if part == 0 else sr.at[:, :, i]
                if delta == 0:
                    ref = sp.at[:, i, 0] if part == 0 else sr.at[:, :, i, 0]
                sem = returned(part, i)
                pl.when(valid(group + delta))(remote(ref, ref, sem, sem, across).wait_send)

    def close():
        ref = dq.at[0]
        remote(ref, ref, gsem.at[0], gsem.at[1], across).wait()
        pltpu.make_async_copy(ref, ref, gsem.at[2]).wait()
        pltpu.make_async_copy(fb, fb, fsem.at[0]).wait()

    half = members * rrows
    lanes = 2 * half
    prompt_blocks = kp.shape[2] // block
    resp_blocks = kr.shape[3] // block
    factor = SCALE * LOG2E
    lane = lax.broadcasted_iota(jnp.int32, (1, lanes), 1)
    row_of = lax.rem(lane, rrows)
    first_row = device(group, 0, core) * rrows
    positions = first_row + row_of + jnp.where(lane < half, 0, 2 * rrows)
    row_iota = lax.broadcasted_iota(jnp.int32, (rrows, 1), 0)
    nt = (((1,), (1,)), ((), ()))

    def key_rows(j):
        return pl.ds(pl.multiple_of(j * block, block), block)

    def compute(unit, ticks):
        k, b = units[unit]
        length = lengths[b]
        for source in range(2):
            live = first_row + source * 2 * rrows + row_iota < length
            for g in range(members):
                cols = pl.ds((k * members + g) * HEAD_DIM, HEAD_DIM)
                at = pl.ds(source * half + g * rrows, rrows)
                qs[at, :] = quh[0, source, b, :, cols]
                rows = quh[1, source, b, :, cols]
                us[at, :] = jnp.where(live, rows, jnp.zeros_like(rows))
        m_buf[...] = jnp.full_like(m_buf, -jnp.inf)
        l_buf[...] = jnp.zeros_like(l_buf)
        e_buf[...] = jnp.zeros_like(e_buf)
        qt_buf[...] = jnp.zeros_like(qt_buf)
        ticks(0)

        def scores(keys, at, j, causal):
            s = lax.dot_general(keys, qs[...], nt, preferred_element_type=jnp.float32)
            if causal:
                s = jnp.where(kpos[key_rows(j), :] <= positions, s, -jnp.inf)
            s_buf[at, :] = s
            m_buf[...] = jnp.maximum(m_buf[...], jnp.max(s, axis=0, keepdims=True))

        @pl.loop(0, prompt_blocks, unroll=True)
        def _(j):
            scores(kp[0, k, key_rows(j), :], key_rows(j), j, False)

        ticks(1)

        @pl.loop(0, resp_blocks, unroll=True)
        def _(j):
            scores(kr[0, k, b, key_rows(j), :], key_rows(prompt_blocks + j), j, True)

        ticks(2)
        shift = m_buf[...] * factor

        def weights(vals, at):
            p = jnp.exp2(s_buf[at, :] * factor - shift)
            d = lax.dot_general(vals, us[...], nt, preferred_element_type=jnp.float32)
            l_buf[...] += jnp.sum(p, axis=0, keepdims=True)
            e_buf[...] += jnp.sum(p * d, axis=0, keepdims=True)
            s_buf[at, :] = p
            d_buf[at, :] = d

        @pl.loop(0, prompt_blocks, unroll=True)
        def _(j):
            weights(kp[1, k, key_rows(j), :], key_rows(j))

        ticks(3)

        @pl.loop(0, resp_blocks, unroll=True)
        def _(j):
            weights(kr[1, k, b, key_rows(j), :], key_rows(prompt_blocks + j))

        ticks(4)
        inverse = 1.0 / l_buf[...]
        delta = e_buf[...] * inverse

        def grads(keys, at):
            p = s_buf[at, :] * inverse
            ds = (p * (d_buf[at, :] - delta)).astype(jnp.bfloat16)
            dv = jnp.dot(p.astype(jnp.bfloat16), us[...], preferred_element_type=jnp.float32)
            dk = jnp.dot(ds, qs[...], preferred_element_type=jnp.float32) * SCALE
            qt_buf[...] += jnp.dot(keys.T, ds, preferred_element_type=jnp.float32)
            return dk, dv

        @pl.loop(0, prompt_blocks, unroll=True)
        def _(j):
            at = key_rows(j)
            pair = grads(kp[0, k, at, :], at)
            for kind in range(2):
                if b == 0:
                    tp[kind, k, at, :] = pair[kind]
                else:
                    tp[kind, k, at, :] += pair[kind]

        ticks(5)

        @pl.loop(0, resp_blocks, unroll=True)
        def _(j):
            at = key_rows(j)
            pair = grads(kr[0, k, b, at, :], key_rows(prompt_blocks + j))
            for kind in range(2):
                tr[kind, k, b, at, :] = pair[kind]

        ticks(6)
        result = (qt_buf[...].T * SCALE).astype(jnp.bfloat16)
        for source in range(2):
            for g in range(members):
                start = source * half + g * rrows
                dq[source, b, :, pl.ds((k * members + g) * HEAD_DIM, HEAD_DIM)] = result[
                    start : start + rrows
                ]
        cols = pl.ds(k * span, span)
        to = query_columns(side, k)
        remote(
            dq.at[1 - side, b, :, cols], gq.at[b, :, to], gsem.at[0], gsem.at[1], across
        ).start()
        pltpu.make_async_copy(dq.at[side, b, :, cols], gq.at[b, :, to], gsem.at[2]).start()

    def needs(unit):
        k, b = units[unit]
        return [(k, 0), (k, 1)] if b == 0 else [(k, 2)]

    def yields(unit):
        k, b = units[unit]
        return [(k, 1)] if b == 0 else [(k, 0), (k, 2)]

    def ready(unit):
        k, b = units[unit]
        for pair in needs(unit):
            shared(*pair).wait_recv()
        query_crossing(k, b, 1 - side).wait_recv()

    last = len(units) - 1
    for pair in needs(0):
        cross(*pair)
    landed(kp.at[:, :, side_rows(0, side), :], 2)
    landed(kr.at[:, :, :, side_rows(1, side), :], 3)
    for pair in needs(0):
        fan(*pair)
    for pair in needs(1):
        cross(*pair)
    landed(quf, 4)
    query_cross(*units[0])
    for unit in range(2, last + 1):
        for pair in needs(unit):
            cross(*pair)
    for unit in range(1, last + 1):
        query_cross(*units[unit])
    arrive(0, 0)
    fan(0, 2)
    arrive(0, 1)
    for pair in needs(2):
        fan(*pair)
    landed(quh.at[:, side], 5)
    ready(0)
    for unit in range(last + 1):
        k, b = units[unit]

        def ticks(at, unit=unit, k=k, b=b):
            if at == 2 and unit + 3 <= last:
                for pair in needs(unit + 3):
                    fan(*pair)
            if at == 4 and unit < last:
                for pair in needs(unit + 1):
                    arrive(*pair)
            if at == 2 and unit > 0:
                for pair in yields(unit - 1):
                    push(*pair)
            if at == 5 and b == 1:
                meet(k, 0)
            if at == 6:
                meet(k, b + 1)
                if unit == last:
                    push(k, 0)

        compute(unit, ticks)
        if unit < last:
            ready(unit + 1)
    for pair in yields(last):
        if pair[1] > 0:
            push(*pair)
    for unit in range(last + 1):
        for pair in yields(unit):
            finish(*pair)
    drain()
    close()


def key_block(prompt, resp):
    size = 256
    while prompt % size or resp % size:
        size //= 2
    return size


def chunks_of(array):
    return 4 if array.size > 1 << 18 else 1


def settle_kernel(*refs):
    count = (len(refs) - 2) // 4
    sources, targets = refs[:count], refs[count : 2 * count]
    holds, wides = refs[2 * count : 3 * count], refs[3 * count : 4 * count]
    taken, given = refs[4 * count :]
    pieces = []
    for source, target, hold, wide in zip(sources, targets, holds, wides):
        chunks = chunks_of(source)
        step = source.shape[-1] // chunks
        for c in range(chunks):
            cut = (slice(None),) * (len(source.shape) - 1) + (pl.ds(c * step, step),)
            i = len(pieces)
            taking = pltpu.make_async_copy(source.at[cut], hold.at[cut], taken.at[i])
            taking.start()
            giving = pltpu.make_async_copy(wide.at[cut], target.at[cut], given.at[i])
            pieces.append((taking, giving, hold, wide, cut))
    for taking, giving, hold, wide, cut in pieces:
        taking.wait()
        wide[cut] = hold[cut].astype(wide.dtype)
        giving.start()
    for piece in pieces:
        piece[1].wait()


def settle(*arrays):
    hbm = pl.BlockSpec(memory_space=pl.ANY)
    dma = pltpu.SemaphoreType.DMA
    pieces = sum(chunks_of(x) for x in arrays)
    return pl.pallas_call(
        settle_kernel,
        out_shape=tuple(jax.ShapeDtypeStruct(x.shape, jnp.float32) for x in arrays),
        in_specs=[hbm] * len(arrays),
        out_specs=(hbm,) * len(arrays),
        scratch_shapes=[pltpu.VMEM(x.shape, x.dtype) for x in arrays]
        + [pltpu.VMEM(x.shape, jnp.float32) for x in arrays]
        + [dma((pieces,)), dma((pieces,))],
        compiler_params=pltpu.CompilerParams(vmem_limit_bytes=60 * MIB),
        name="settle",
    )(*arrays)


def local(prompt_keys, prompt_values, queries, resp_keys, resp_values, cotangent, lengths):
    devices = lax.axis_size("ctx")
    groups = devices // 4
    prows, columns = prompt_keys.shape
    rows, wide = queries.shape[1], queries.shape[2] // 2
    heads = columns // 2 // HEAD_DIM
    prompt, resp = prows * devices, rows * devices
    smem = pl.BlockSpec(memory_space=pltpu.SMEM)
    hbm = pl.BlockSpec(memory_space=pl.ANY)
    shape = jax.ShapeDtypeStruct
    bf16, f32 = jnp.bfloat16, jnp.float32
    vmem, dma = pltpu.VMEM, pltpu.SemaphoreType.DMA
    block = key_block(prompt, resp)
    lanes = 2 * rows * (wide // HEAD_DIM) // heads
    total = prompt + resp
    both, one = len(offsets(groups, (1, -1))), len(offsets(groups, (1,)))
    outs = pl.pallas_call(
        functools.partial(fused_kernel, groups, block),
        out_shape=(
            shape((2, rows, 2 * wide), bf16),
            shape((2, rows, columns), f32), shape((2, rows, columns), f32),
            shape((prows, columns), f32), shape((prows, columns), f32),
        ),
        in_specs=[smem] + [hbm] * 6,
        out_specs=(hbm,) * 5,
        scratch_shapes=[
            vmem((2, heads, prompt, HEAD_DIM), bf16),
            vmem((2, heads, 2, resp, HEAD_DIM), bf16),
            vmem((heads, 2, prows, HEAD_DIM), bf16),
            vmem((heads, 2, 2, rows, HEAD_DIM), bf16),
            vmem((resp, 1), jnp.int32),
            vmem((2, 2, 2, rows, wide), bf16), vmem((2, 2, rows, wide), bf16),
            vmem((lanes, HEAD_DIM), bf16), vmem((lanes, HEAD_DIM), bf16),
            vmem((total, lanes), f32), vmem((total, lanes), f32),
            vmem((HEAD_DIM, lanes), f32),
            vmem((1, lanes), f32), vmem((1, lanes), f32), vmem((1, lanes), f32),
            vmem((2, heads, prompt, HEAD_DIM), f32),
            vmem((2, heads, 2, resp, HEAD_DIM), f32),
            vmem((2, heads, prompt // 2, HEAD_DIM), f32),
            vmem((2, heads, 2, resp // 2, HEAD_DIM), f32),
            vmem((heads, both + 1, 2, 2, prows, HEAD_DIM), bf16),
            vmem((heads, 2, one + 1, 2, 2, rows, HEAD_DIM), bf16),
            vmem((heads, 2, groups, 2, prows, HEAD_DIM), bf16),
            vmem((heads, 2, 2, groups, 2, rows, HEAD_DIM), bf16),
            vmem((heads, 2, 2, prows + 2 * rows, HEAD_DIM), f32),
            vmem((2, 2, rows, wide), bf16),
            dma((6,)), dma((2,)), dma((3, heads)), dma((1,)), dma((heads, 2)),
            dma((heads, both)), dma((heads, one)), dma((3, heads, groups)), dma((3,)),
            dma((2,)), dma((3, heads)), dma((2,)), dma((3, heads)),
            dma((both + 1,)), dma((one + 1,)), dma((3, heads, groups)), dma((1,)), dma((3,)),
        ],
        compiler_params=pltpu.CompilerParams(
            collective_id=0, has_side_effects=True, vmem_limit_bytes=60 * MIB
        ),
        name="fused",
    )(lengths, prompt_keys, prompt_values, resp_keys, resp_values, queries, cotangent)
    return settle(*outs)


def solution(mesh):
    placed = (
        P(("pairs", "ctx"), None),
        P(("pairs", "ctx"), None),
        P("pairs", "ctx", None),
        P("pairs", "ctx", None),
        P("pairs", "ctx", None),
        P("pairs", "ctx", None),
        P("pairs"),
    )
    return jax.shard_map(
        local,
        mesh=mesh,
        in_specs=placed,
        out_specs=(
            P("pairs", "ctx", None),
            P("pairs", "ctx", None),
            P("pairs", "ctx", None),
            P(("pairs", "ctx"), None),
            P(("pairs", "ctx"), None),
        ),
        check_vma=False,
    )
```

time: 71.3 us -> 57.3 us (0.80)
  Pallas kernels: 70.4 us -> 56.3 us
    pallas_call x1, Pallas kernels: 67.8 us -> 53.9 us  [local(): pl.pallas_call(functools.partial(fused_kernel, groups, block), out_shape=...]
where the time goes in v2:
time: 57.3 us; the launch traced here: 57.1 us
  Pallas kernels  56.3 us (98%)
  between operations  0.8 us (1%)
    pallas_call x1, Pallas kernels, local(): pl.pallas_call(functools.partial(fused_kernel, groups, block), out_shape=...  53.9 us
    pallas_call x1, Pallas kernels, settle(): pl.pallas_call(settle_kernel, out_shape=tuple((jax.ShapeDtypeStruct(x.sha...  2.39 us

profile of v2, /device:TPU:0, one launch (start us, length us, event | category | flops | bytes accessed | tf_op | source)
XLA Modules:
  0.0 57.1 jit_solution(9261562575637602295)
XLA Ops:
  0.6 53.9 %fused.1 = (bf16[2,48,4096]{2,1,0:T(8,128)(2,1)}, f32[2,48,512]{2,1,0:T(8,128)}, f32[2,48,512]{2,1,0:T(8,128)}, f32[32,512]{1,0:T(8,128)}, f32[32,512]{1,0:T(8,128)}) custom-call(s32[2]{0:T(128)} %lengths.1, bf16[32,512]{1,0:T(8,128)(2,1)} %pk.1, bf16[32,512]{1,0:T(8,128)(2,1)} %pv.1, bf16[2,48,512]{2,1,0:T(8,128)(2,1)} %rk.1, bf16[2,48,512]{2,1,0:T(8,128)(2,1)} %rv.1, ...), custom_call_target="tpu_custom_call" | custom-call | tf_op jit(solution)/shard_map/fused/pallas_call | solution.py:595
  54.6 2.4 %settle.1 = (f32[2,48,4096]{2,1,0:T(8,128)}, f32[2,48,512]{2,1,0:T(8,128)}, f32[2,48,512]{2,1,0:T(8,128)}, f32[32,512]{1,0:T(8,128)}, f32[32,512]{1,0:T(8,128)}) custom-call(bf16[2,48,4096]{2,1,0:T(8,128)(2,1)} %get-tuple-element.10.refs_0_, f32[2,48,512]{2,1,0:T(8,128)} %get-tuple-element.11.refs_1_, f32[2,48,512]{2,1,0:T(8,128)} %get-tuple-element.12.refs_2_, ...), custom_call_target="tpu_custom_call" | custom-call | tf_op jit(solution)/shard_map/settle/pallas_call | solution.py:566

commit v3 on v2

--- a/solution.py
+++ b/solution.py
@@ -11,7 +11,7 @@
 SCALE = HEAD_DIM ** (-0.5)
 LOG2E = 1.4426950408889634
 MIB = 1024 * 1024
-RELAYED = 3
+FAR = 3
 
 
 def remote(src, dst, send, recv, device):
@@ -26,7 +26,7 @@
 
 
 def offsets(groups, signs):
-    order = [2, 1, 3] + list(range(4, groups))
+    order = [3, 2, 1] + list(range(4, groups))
     return [sign * far for far in order if far < groups for sign in signs]
 
 
@@ -34,8 +34,8 @@
     groups, block, lengths, pk, pv, rk, rv, q, u,
     gq, grk, grv, gpk, gpv,
     kp, kr, bp, br, kpos, quh, quf, qs, us, s_buf, d_buf, qt_buf, m_buf, l_buf, e_buf,
-    tp, tr, xp, xr, sp, sr, rp, rr, fb, dq,
-    local_sem, ysend, yrecv, qsend, qrecv, asend_p, asend_r, arecv, bsend, dsend, drecv,
+    tp, tr, xp, xr, sp, sr, rp, rr, lp, lr, fb, dq,
+    local_sem, ysend, yrecv, qsend, qrecv, asend_p, asend_r, arecv, bsend, lrecv, dsend, drecv,
     csend, crecv, zsend_p, zsend_r, zrecv, fsem, gsem,
 ):
     me = lax.axis_index("ctx")
@@ -46,6 +46,7 @@
 
     partner = device(group, side, 1 - core)
     across = device(group, 1 - side, core)
+    onward, back = me + 4, me - 4
     prows, rrows = pk.shape[0], rk.shape[1]
     heads = kp.shape[1]
     wide = q.shape[2] // 2
@@ -102,9 +103,6 @@
     def valid(where):
         return jnp.logical_and(where >= 0, where < groups)
 
-    def relays(k, delta):
-        return k == 0 and abs(delta) == RELAYED
-
     units = [(k, b) for k in range(heads) for b in range(2)]
     order = [(k, part) for k in range(heads) for part in parts]
 
@@ -114,11 +112,13 @@
             def _(c=c, where=where):
                 empty = jnp.zeros((2, heads, 2, 2 * rrows, HEAD_DIM), kr.dtype)
                 kr[:, :, :, pl.ds((c * groups + where) * 2 * rrows, 2 * rrows), :] = empty
-    for ref in (rp, rr):
+    for ref in (rp, rr, lp, lr):
         ref[...] = jnp.zeros_like(ref)
 
     barrier = pltpu.get_barrier_semaphore()
-    peers = [partner, across] + [device((group + i) % groups, side, core) for i in range(1, groups)]
+    peers = [partner, across] + [
+        device((group + i) % groups, y, core) for i in range(1, groups) for y in range(2)
+    ]
     for other in peers:
         pl.semaphore_signal(
             barrier, inc=1, device_id={"ctx": other}, device_id_type=pl.DeviceIdType.MESH
@@ -159,17 +159,10 @@
     landed(bp, 0)
     landed(br, 1)
 
-    def crossing(k, part, y):
-        ref = pick((kp, kr), k, part).at[:, side_rows(part, y), :]
-        return remote(ref, ref, ysend.at[min(part, 1)], yrecv.at[part, k], across)
-
-    def cross(k, part):
-        for kind in range(2):
-            remote(
-                stack((bp, br), k, part).at[kind],
-                pick((kp, kr), k, part).at[kind, side_rows(part, side), :],
-                ysend.at[min(part, 1)], yrecv.at[part, k], across,
-            ).start()
+    def cross(k, part, kind, y=side):
+        src = stack((bp, br), k, part).at[kind]
+        dst = pick((kp, kr), k, part).at[kind, side_rows(part, y), :]
+        return remote(src, dst, ysend.at[min(part, 1)], yrecv.at[kind, part, k], across)
 
     def query_crossing(k, b, y):
         ref = quh.at[:, y, b, :, pl.ds(k * span, span)]
@@ -183,39 +176,66 @@
                 qsend.at[0], qrecv.at[k, b], across,
             ).start()
 
-    def shared(k, part):
-        ref = pick((kp, kr), k, part).at[:, core_rows(part, core), :]
-        return remote(ref, ref, dsend.at[min(part, 1)], drecv.at[part, k], partner)
-
-    def fanned(k, part, i):
-        return asend_p.at[k, i] if part == 0 else asend_r.at[k, i]
-
-    def fan(k, part):
-        crossing(k, part, 1 - side).wait_recv()
-        ref = pick((kp, kr), k, part).at[:, block_rows(part, core, group), :]
+    def shared(k, part, kind):
+        ref = pick((kp, kr), k, part).at[kind, core_rows(part, core), :]
+        return remote(ref, ref, dsend.at[min(part, 1)], drecv.at[kind, part, k], partner)
+
+    def fanned(part, i):
+        return asend_p.at[i] if part == 0 else asend_r.at[i]
+
+    def fan(k, part, kind):
+        cross(k, part, kind, 1 - side).wait_recv()
+        ref = pick((kp, kr), k, part).at[kind, block_rows(part, core, group), :]
         for i, delta in enumerate(offsets(groups, signs_out(part))):
-            if relays(k, delta):
+            if delta == FAR:
                 continue
             to = group + delta
             copy = remote(
-                ref, ref, fanned(k, part, i), arecv.at[part, k, group], device(to, side, core)
+                ref, ref, fanned(part, i), arecv.at[kind, part, k, group], device(to, side, core)
             )
             pl.when(valid(to))(copy.start)
 
-    def arrive(k, part):
+    def spread(k, part, kind):
+        near = pick((kp, kr), k, part).at[kind, side_rows(part, side), :]
+        far = stack((bp, br), k, part).at[kind]
+        for i, delta in enumerate(offsets(groups, signs_out(part))):
+            if delta == FAR:
+                continue
+            to = group + delta
+            sem, got = fanned(part, i), arecv.at[kind, part, k, group]
+
+            @pl.when(valid(to))
+            def _(to=to, sem=sem, got=got):
+                remote(near, near, sem, got, device(to, side, core)).start()
+                remote(far, near, sem, got, device(to, 1 - side, core)).start()
+
+    def came(k, part, kind, origin):
+        ref = pick((kp, kr), k, part).at[kind, block_rows(part, core, origin), :]
+        return remote(ref, ref, bsend.at[min(part, 1)], arecv.at[kind, part, k, origin], onward)
+
+    def relay(k, part, kind):
+        if groups <= FAR:
+            return
+        origin = group - FAR + 1
+        copy = came(k, part, kind, origin)
+
+        @pl.when(jnp.logical_and(origin >= 0, group + 1 < groups))
+        def _():
+            copy.wait_recv()
+            copy.start()
+
+    def arrive(k, part, kind):
+        if (k, part) in spread_parts and kind == 0:
+            cross(k, part, kind, 1 - side).wait_recv()
         for delta in sorted(offsets(groups, signs_out(part)), key=abs):
             origin = group - delta
-            step = 1 if delta > 0 else -1
-            ref = pick((kp, kr), k, part).at[:, block_rows(part, core, origin), :]
-            copy = remote(ref, ref, bsend.at[0], arecv.at[part, k, origin], partner)
-            pl.when(valid(origin))(copy.wait_recv)
-            if k == 0 and abs(delta) == RELAYED - 1:
-                copy = remote(
-                    ref, ref, bsend.at[2 if part > 0 else (1 - step) // 2],
-                    arecv.at[part, k, origin], device(group + step, side, core),
-                )
-                pl.when(jnp.logical_and(valid(origin), valid(group + step)))(copy.start)
-        shared(k, part).start()
+            waits = valid(origin)
+            if delta == FAR - 1 and groups > FAR:
+                waits = jnp.logical_and(waits, group + 1 >= groups)
+            pl.when(waits)(came(k, part, kind, origin).wait_recv)
+        shared(k, part, kind).start()
+
+    spread_parts = ((0, 0), (0, 1))
 
     def met(k, part):
         ref = pick((tp, tr), k, part).at[:, core_rows(part, 1 - core), :]
@@ -237,27 +257,38 @@
     def returned(part, i):
         return zsend_p.at[i] if part == 0 else zsend_r.at[i]
 
-    def push(k, part):
-        met(k, part).wait_recv()
+    def push(k, part, gathers):
         size = size_of(part)
+        passing = stack((lp, lr), k, part)
         for i, delta in enumerate(returns(part)):
             to = group + delta
+            if (delta == 1 - FAR and groups > FAR) != gathers:
+                continue
             out = stack((sp, sr), k, part).at[i]
-            sides = range(2) if delta else (1 - side,)
-            copies = [
-                remote(
-                    out.at[y], stack((rp, rr), k, part).at[side, group], returned(part, i),
-                    zrecv.at[part, k, group], device(to, y, core),
-                )
-                for y in sides
-            ]
+            if delta == -FAR:
+                copies = [remote(out, passing, returned(part, i), lrecv.at[part, k], back)]
+            else:
+                sides = range(2) if delta else (1 - side,)
+                copies = [
+                    remote(
+                        out.at[y], stack((rp, rr), k, part).at[side, group], returned(part, i),
+                        zrecv.at[part, k, group], device(to, y, core),
+                    )
+                    for y in sides
+                ]
+            if gathers:
+                copy = remote(out, passing, returned(part, i), lrecv.at[part, k], back)
+                pl.when(jnp.logical_and(to >= 0, group + 1 < groups))(copy.wait_recv)
 
             @pl.when(valid(to))
             def _(to=to, out=out, copies=copies):
                 for kind in range(2):
-                    value = total(kind, k, part, to).astype(jnp.bfloat16)
+                    value = total(kind, k, part, to)
                     for y in range(2):
-                        out[y, kind] = value[y * size : (y + 1) * size]
+                        piece = value[y * size : (y + 1) * size]
+                        if gathers:
+                            piece = piece + passing[y, kind].astype(jnp.float32)
+                        out[y, kind] = piece.astype(jnp.bfloat16)
                 for copy in copies:
                     copy.start()
 
@@ -267,9 +298,11 @@
         got = stack((rp, rr), k, part)
         size = size_of(part)
         for delta in returns(part):
+            if delta == -FAR:
+                continue
             origin = group - delta
             slot = got.at[:, origin] if delta else got.at[0, origin]
-            copy = remote(slot, slot, bsend.at[0], zrecv.at[part, k, origin], partner)
+            copy = remote(slot, slot, fanned(part, 0), zrecv.at[part, k, origin], partner)
             pl.when(valid(origin))(copy.wait_recv)
         rows = pl.ds(starts[part], size)
         near = at_row(group * 2 * size + side * size, size)
@@ -300,31 +333,23 @@
         remote(ref, ref, csend.at[1], csend.at[1], partner).wait_send()
         for part in range(2):
             for i, delta in enumerate(offsets(groups, signs_out(part))):
-                refs = []
-                for k in range(heads):
-                    if not relays(k, delta):
-                        if part == 0:
-                            ref = kp.at[:, k, block_rows(0, core, group), :]
-                        else:
-                            ref = kr.at[:, k, :, block_rows(1, core, group), :]
-                        refs.append((ref, fanned(k, part, i)))
-
-                @pl.when(valid(group + delta))
-                def _(refs=refs):
-                    for ref, sem in refs:
-                        remote(ref, ref, sem, sem, across).wait_send()
-
-                if abs(delta) == RELAYED - 1:
-                    step = 1 if delta > 0 else -1
-                    origin = group - delta
-                    if part == 0:
-                        ref = kp.at[:, 0, block_rows(0, core, origin), :]
-                    else:
-                        ref = kr.at[:, 0, :, block_rows(1, core, origin), :]
-                    sem = bsend.at[2 if part > 0 else (1 - step) // 2]
-                    pl.when(jnp.logical_and(valid(origin), valid(group + step)))(
-                        remote(ref, ref, sem, sem, across).wait_send
-                    )
+                if part == 0:
+                    ref = kp.at[:, :, block_rows(0, core, group), :]
+                else:
+                    ref = kr.at[:, :, :, block_rows(1, core, group), :]
+                sem = fanned(part, i)
+                if delta != FAR:
+                    pl.when(valid(group + delta))(remote(ref, ref, sem, sem, across).wait_send)
+                    continue
+                origin = group - FAR + 1
+                if part == 0:
+                    ref = kp.at[:, :, block_rows(0, core, origin), :]
+                else:
+                    ref = kr.at[:, :, :, block_rows(1, core, origin), :]
+                sem = bsend.at[part]
+                pl.when(jnp.logical_and(origin >= 0, group + 1 < groups))(
+                    remote(ref, ref, sem, sem, across).wait_send
+                )
             for i, delta in enumerate(returns(part)):
                 ref = sp.at[:, i] if part == 0 else sr.at[:, :, i]
                 if delta == 0:
@@ -465,58 +490,91 @@
     def ready(unit):
         k, b = units[unit]
         for pair in needs(unit):
-            shared(*pair).wait_recv()
+            shared(*pair, 0).wait_recv()
         query_crossing(k, b, 1 - side).wait_recv()
 
     last = len(units) - 1
-    for pair in needs(0):
-        cross(*pair)
     landed(kp.at[:, :, side_rows(0, side), :], 2)
     landed(kr.at[:, :, :, side_rows(1, side), :], 3)
-    for pair in needs(0):
-        fan(*pair)
+    for pair in spread_parts:
+        spread(*pair, 0)
+        cross(*pair, 0).start()
+    for pair in spread_parts:
+        cross(*pair, 1).start()
     for pair in needs(1):
-        cross(*pair)
+        for kind in range(2):
+            cross(*pair, kind).start()
     landed(quf, 4)
     query_cross(*units[0])
     for unit in range(2, last + 1):
         for pair in needs(unit):
-            cross(*pair)
+            for kind in range(2):
+                cross(*pair, kind).start()
     for unit in range(1, last + 1):
         query_cross(*units[unit])
-    arrive(0, 0)
-    fan(0, 2)
-    arrive(0, 1)
-    for pair in needs(2):
-        fan(*pair)
+    for pair in spread_parts:
+        fan(*pair, 1)
+    for pair in spread_parts:
+        relay(*pair, 0)
+    for kind in range(2):
+        fan(0, 2, kind)
+    for pair in spread_parts:
+        arrive(*pair, 0)
+    for pair in spread_parts:
+        relay(*pair, 1)
     landed(quh.at[:, side], 5)
     ready(0)
     for unit in range(last + 1):
         k, b = units[unit]
 
         def ticks(at, unit=unit, k=k, b=b):
-            if at == 2 and unit + 3 <= last:
+            if at == 0 and unit < last:
+                for kind in range(2):
+                    for pair in needs(unit + 1):
+                        relay(*pair, kind)
+            if unit == 0 and at == 1:
+                for pair in needs(2):
+                    for kind in range(2):
+                        fan(*pair, kind)
+                arrive(0, 0, 1)
+            if at == 2:
+                if unit == 0:
+                    arrive(0, 1, 1)
+                for pair in needs(unit):
+                    shared(*pair, 1).wait_recv()
+            if at == 3 and unit + 3 <= last:
                 for pair in needs(unit + 3):
-                    fan(*pair)
-            if at == 4 and unit < last:
+                    for kind in range(2):
+                        fan(*pair, kind)
+            if at in (4, 5) and unit < last:
                 for pair in needs(unit + 1):
-                    arrive(*pair)
+                    arrive(*pair, at - 4)
             if at == 2 and unit > 0:
                 for pair in yields(unit - 1):
-                    push(*pair)
+                    met(*pair).wait_recv()
+                    push(*pair, False)
+            if at == 2 and unit > 1:
+                for pair in yields(unit - 2):
+                    push(*pair, True)
             if at == 5 and b == 1:
                 meet(k, 0)
             if at == 6:
                 meet(k, b + 1)
                 if unit == last:
-                    push(k, 0)
+                    for pair in yields(unit - 1):
+                        push(*pair, True)
+                    met(k, 0).wait_recv()
+                    push(k, 0, False)
 
         compute(unit, ticks)
         if unit < last:
             ready(unit + 1)
     for pair in yields(last):
         if pair[1] > 0:
-            push(*pair)
+            met(*pair).wait_recv()
+            push(*pair, False)
+    for pair in yields(last):
+        push(*pair, True)
     for unit in range(last + 1):
         for pair in yields(unit):
             finish(*pair)
@@ -620,11 +678,13 @@
             vmem((heads, 2, one + 1, 2, 2, rows, HEAD_DIM), bf16),
             vmem((heads, 2, groups, 2, prows, HEAD_DIM), bf16),
             vmem((heads, 2, 2, groups, 2, rows, HEAD_DIM), bf16),
+            vmem((heads, 2, 2, prows, HEAD_DIM), bf16),
+            vmem((heads, 2, 2, 2, rows, HEAD_DIM), bf16),
             vmem((heads, 2, 2, prows + 2 * rows, HEAD_DIM), f32),
             vmem((2, 2, rows, wide), bf16),
-            dma((6,)), dma((2,)), dma((3, heads)), dma((1,)), dma((heads, 2)),
-            dma((heads, both)), dma((heads, one)), dma((3, heads, groups)), dma((3,)),
-            dma((2,)), dma((3, heads)), dma((2,)), dma((3, heads)),
+            dma((6,)), dma((2,)), dma((2, 3, heads)), dma((1,)), dma((heads, 2)),
+            dma((both,)), dma((one,)), dma((2, 3, heads, groups)), dma((2,)), dma((3, heads)),
+            dma((2,)), dma((2, 3, heads)), dma((2,)), dma((3, heads)),
             dma((both + 1,)), dma((one + 1,)), dma((3, heads, groups)), dma((1,)), dma((3,)),
         ],
         compiler_params=pltpu.CompilerParams(

time: 57.3 us -> 51.6 us (0.901)
  Pallas kernels: 56.3 us -> 50.7 us
    pallas_call x1, Pallas kernels: 53.9 us -> 48.3 us  [local(): pl.pallas_call(functools.partial(fused_kernel, groups, block), out_shape=...]
where the time goes in v3:
time: 51.6 us; the launch traced here: 51.5 us
  Pallas kernels  50.7 us (98%)
  between operations  0.8 us (2%)
    pallas_call x1, Pallas kernels, local(): pl.pallas_call(functools.partial(fused_kernel, groups, block), out_shape=...  48.3 us
    pallas_call x1, Pallas kernels, settle(): pl.pallas_call(settle_kernel, out_shape=tuple((jax.ShapeDtypeStruct(x.sha...  2.39 us

profile of v3, /device:TPU:0, one launch (start us, length us, event | category | flops | bytes accessed | tf_op | source)
XLA Modules:
  0.0 51.5 jit_solution(5042128001533996750)
XLA Ops:
  0.6 48.3 %fused.1 = (bf16[2,48,4096]{2,1,0:T(8,128)(2,1)}, f32[2,48,512]{2,1,0:T(8,128)}, f32[2,48,512]{2,1,0:T(8,128)}, f32[32,512]{1,0:T(8,128)}, f32[32,512]{1,0:T(8,128)}) custom-call(s32[2]{0:T(128)} %lengths.1, bf16[32,512]{1,0:T(8,128)(2,1)} %pk.1, bf16[32,512]{1,0:T(8,128)(2,1)} %pv.1, bf16[2,48,512]{2,1,0:T(8,128)(2,1)} %rk.1, bf16[2,48,512]{2,1,0:T(8,128)(2,1)} %rv.1, ...), custom_call_target="tpu_custom_call" | custom-call | tf_op jit(solution)/shard_map/fused/pallas_call | solution.py:653
  48.9 2.4 %settle.1 = (f32[2,48,4096]{2,1,0:T(8,128)}, f32[2,48,512]{2,1,0:T(8,128)}, f32[2,48,512]{2,1,0:T(8,128)}, f32[32,512]{1,0:T(8,128)}, f32[32,512]{1,0:T(8,128)}) custom-call(bf16[2,48,4096]{2,1,0:T(8,128)(2,1)} %get-tuple-element.10.refs_0_, f32[2,48,512]{2,1,0:T(8,128)} %get-tuple-element.11.refs_1_, f32[2,48,512]{2,1,0:T(8,128)} %get-tuple-element.12.refs_2_, ...), custom_call_target="tpu_custom_call" | custom-call | tf_op jit(solution)/shard_map/settle/pallas_call | solution.py:624

commit v4 on v3

--- a/solution.py
+++ b/solution.py
@@ -164,17 +164,12 @@
         dst = pick((kp, kr), k, part).at[kind, side_rows(part, y), :]
         return remote(src, dst, ysend.at[min(part, 1)], yrecv.at[kind, part, k], across)
 
-    def query_crossing(k, b, y):
-        ref = quh.at[:, y, b, :, pl.ds(k * span, span)]
-        return remote(ref, ref, qsend.at[0], qrecv.at[k, b], across)
-
-    def query_cross(k, b):
+    def query_cross(i, k, b, y=side):
         cols = pl.ds(k * span, span)
-        for i in range(2):
-            remote(
-                quf.at[i, b, :, cols], quh.at[i, side, b, :, cols],
-                qsend.at[0], qrecv.at[k, b], across,
-            ).start()
+        return remote(
+            quf.at[i, b, :, cols], quh.at[i, y, b, :, cols],
+            qsend.at[0], qrecv.at[i, k, b], across,
+        )
 
     def shared(k, part, kind):
         ref = pick((kp, kr), k, part).at[kind, core_rows(part, core), :]
@@ -260,9 +255,13 @@
     def push(k, part, gathers):
         size = size_of(part)
         passing = stack((lp, lr), k, part)
+        more = group + 1 < groups
         for i, delta in enumerate(returns(part)):
             to = group + delta
-            if (delta == 1 - FAR and groups > FAR) != gathers:
+            cond = valid(to)
+            if delta == 1 - FAR and groups > FAR:
+                cond = jnp.logical_and(cond, more if gathers else jnp.logical_not(more))
+            elif gathers:
                 continue
             out = stack((sp, sr), k, part).at[i]
             if delta == -FAR:
@@ -276,12 +275,12 @@
                     )
                     for y in sides
                 ]
-            if gathers:
-                copy = remote(out, passing, returned(part, i), lrecv.at[part, k], back)
-                pl.when(jnp.logical_and(to >= 0, group + 1 < groups))(copy.wait_recv)
-
-            @pl.when(valid(to))
-            def _(to=to, out=out, copies=copies):
+            wait = remote(out, passing, returned(part, i), lrecv.at[part, k], back)
+
+            @pl.when(cond)
+            def _(to=to, out=out, copies=copies, wait=wait):
+                if gathers:
+                    wait.wait_recv()
                 for kind in range(2):
                     value = total(kind, k, part, to)
                     for y in range(2):
@@ -382,13 +381,10 @@
         k, b = units[unit]
         length = lengths[b]
         for source in range(2):
-            live = first_row + source * 2 * rrows + row_iota < length
             for g in range(members):
                 cols = pl.ds((k * members + g) * HEAD_DIM, HEAD_DIM)
                 at = pl.ds(source * half + g * rrows, rrows)
                 qs[at, :] = quh[0, source, b, :, cols]
-                rows = quh[1, source, b, :, cols]
-                us[at, :] = jnp.where(live, rows, jnp.zeros_like(rows))
         m_buf[...] = jnp.full_like(m_buf, -jnp.inf)
         l_buf[...] = jnp.zeros_like(l_buf)
         e_buf[...] = jnp.zeros_like(e_buf)
@@ -413,6 +409,13 @@
             scores(kr[0, k, b, key_rows(j), :], key_rows(prompt_blocks + j), j, True)
 
         ticks(2)
+        for source in range(2):
+            live = first_row + source * 2 * rrows + row_iota < length
+            for g in range(members):
+                cols = pl.ds((k * members + g) * HEAD_DIM, HEAD_DIM)
+                at = pl.ds(source * half + g * rrows, rrows)
+                rows = quh[1, source, b, :, cols]
+                us[at, :] = jnp.where(live, rows, jnp.zeros_like(rows))
         shift = m_buf[...] * factor
 
         def weights(vals, at):
@@ -491,7 +494,7 @@
         k, b = units[unit]
         for pair in needs(unit):
             shared(*pair, 0).wait_recv()
-        query_crossing(k, b, 1 - side).wait_recv()
+        query_cross(0, k, b, 1 - side).wait_recv()
 
     last = len(units) - 1
     landed(kp.at[:, :, side_rows(0, side), :], 2)
@@ -501,17 +504,23 @@
         cross(*pair, 0).start()
     for pair in spread_parts:
         cross(*pair, 1).start()
-    for pair in needs(1):
+    for kind in range(2):
+        cross(0, 2, kind).start()
+    landed(quf, 4)
+    query_cross(0, *units[0]).start()
+    for kind in range(2):
+        for pair in needs(2):
+            cross(*pair, kind).start()
+    query_cross(1, *units[0]).start()
+    for unit in range(3, last + 1):
         for kind in range(2):
-            cross(*pair, kind).start()
-    landed(quf, 4)
-    query_cross(*units[0])
+            for pair in needs(unit):
+                cross(*pair, kind).start()
+    for i in range(2):
+        query_cross(i, *units[1]).start()
     for unit in range(2, last + 1):
-        for pair in needs(unit):
-            for kind in range(2):
-                cross(*pair, kind).start()
-    for unit in range(1, last + 1):
-        query_cross(*units[unit])
+        for i in range(2):
+            query_cross(i, *units[unit]).start()
     for pair in spread_parts:
         fan(*pair, 1)
     for pair in spread_parts:
@@ -522,26 +531,26 @@
         arrive(*pair, 0)
     for pair in spread_parts:
         relay(*pair, 1)
+    for kind in range(2):
+        for pair in needs(2):
+            fan(*pair, kind)
     landed(quh.at[:, side], 5)
     ready(0)
     for unit in range(last + 1):
         k, b = units[unit]
 
         def ticks(at, unit=unit, k=k, b=b):
-            if at == 0 and unit < last:
+            if at == 0 and unit == 0:
                 for kind in range(2):
-                    for pair in needs(unit + 1):
-                        relay(*pair, kind)
+                    relay(0, 2, kind)
             if unit == 0 and at == 1:
-                for pair in needs(2):
-                    for kind in range(2):
-                        fan(*pair, kind)
                 arrive(0, 0, 1)
             if at == 2:
                 if unit == 0:
                     arrive(0, 1, 1)
                 for pair in needs(unit):
                     shared(*pair, 1).wait_recv()
+                query_cross(1, k, b, 1 - side).wait_recv()
             if at == 3 and unit + 3 <= last:
                 for pair in needs(unit + 3):
                     for kind in range(2):
@@ -560,6 +569,10 @@
                 meet(k, 0)
             if at == 6:
                 meet(k, b + 1)
+                if unit + 2 <= last:
+                    for kind in range(2):
+                        for pair in needs(unit + 2):
+                            relay(*pair, kind)
                 if unit == last:
                     for pair in yields(unit - 1):
                         push(*pair, True)
@@ -682,7 +695,7 @@
             vmem((heads, 2, 2, 2, rows, HEAD_DIM), bf16),
             vmem((heads, 2, 2, prows + 2 * rows, HEAD_DIM), f32),
             vmem((2, 2, rows, wide), bf16),
-            dma((6,)), dma((2,)), dma((2, 3, heads)), dma((1,)), dma((heads, 2)),
+            dma((6,)), dma((2,)), dma((2, 3, heads)), dma((1,)), dma((2, heads, 2)),
             dma((both,)), dma((one,)), dma((2, 3, heads, groups)), dma((2,)), dma((3, heads)),
             dma((2,)), dma((2, 3, heads)), dma((2,)), dma((3, heads)),
             dma((both + 1,)), dma((one + 1,)), dma((3, heads, groups)), dma((1,)), dma((3,)),

time: 51.6 us -> 50.6 us (0.981)
  Pallas kernels: 50.7 us -> 49.6 us
    pallas_call x1, Pallas kernels: 48.3 us -> 47.2 us  [local(): pl.pallas_call(functools.partial(fused_kernel, groups, block), out_shape=...]
where the time goes in v4:
time: 50.6 us; the launch traced here: 50.4 us
  Pallas kernels  49.6 us (98%)
  between operations  0.8 us (2%)
    pallas_call x1, Pallas kernels, local(): pl.pallas_call(functools.partial(fused_kernel, groups, block), out_shape=...  47.2 us
    pallas_call x1, Pallas kernels, settle(): pl.pallas_call(settle_kernel, out_shape=tuple((jax.ShapeDtypeStruct(x.sha...  2.39 us

profile of v4, /device:TPU:0, one launch (start us, length us, event | category | flops | bytes accessed | tf_op | source)
XLA Modules:
  0.0 50.4 jit_solution(13710887061483669177)
XLA Ops:
  0.6 47.2 %fused.1 = (bf16[2,48,4096]{2,1,0:T(8,128)(2,1)}, f32[2,48,512]{2,1,0:T(8,128)}, f32[2,48,512]{2,1,0:T(8,128)}, f32[32,512]{1,0:T(8,128)}, f32[32,512]{1,0:T(8,128)}) custom-call(s32[2]{0:T(128)} %lengths.1, bf16[32,512]{1,0:T(8,128)(2,1)} %pk.1, bf16[32,512]{1,0:T(8,128)(2,1)} %pv.1, bf16[2,48,512]{2,1,0:T(8,128)(2,1)} %rk.1, bf16[2,48,512]{2,1,0:T(8,128)(2,1)} %rv.1, ...), custom_call_target="tpu_custom_call" | custom-call | tf_op jit(solution)/shard_map/fused/pallas_call | solution.py:666
  47.8 2.4 %settle.1 = (f32[2,48,4096]{2,1,0:T(8,128)}, f32[2,48,512]{2,1,0:T(8,128)}, f32[2,48,512]{2,1,0:T(8,128)}, f32[32,512]{1,0:T(8,128)}, f32[32,512]{1,0:T(8,128)}) custom-call(bf16[2,48,4096]{2,1,0:T(8,128)(2,1)} %get-tuple-element.10.refs_0_, f32[2,48,512]{2,1,0:T(8,128)} %get-tuple-element.11.refs_1_, f32[2,48,512]{2,1,0:T(8,128)} %get-tuple-element.12.refs_2_, ...), custom_call_target="tpu_custom_call" | custom-call | tf_op jit(solution)/shard_map/settle/pallas_call | solution.py:637

commit v5 on v4

--- a/solution.py
+++ b/solution.py
@@ -252,7 +252,7 @@
     def returned(part, i):
         return zsend_p.at[i] if part == 0 else zsend_r.at[i]
 
-    def push(k, part, gathers):
+    def push(k, part, gathers, only=None):
         size = size_of(part)
         passing = stack((lp, lr), k, part)
         more = group + 1 < groups
@@ -262,6 +262,8 @@
             if delta == 1 - FAR and groups > FAR:
                 cond = jnp.logical_and(cond, more if gathers else jnp.logical_not(more))
             elif gathers:
+                continue
+            if only is not None and (delta == -FAR) != only:
                 continue
             out = stack((sp, sr), k, part).at[i]
             if delta == -FAR:
@@ -531,9 +533,6 @@
         arrive(*pair, 0)
     for pair in spread_parts:
         relay(*pair, 1)
-    for kind in range(2):
-        for pair in needs(2):
-            fan(*pair, kind)
     landed(quh.at[:, side], 5)
     ready(0)
     for unit in range(last + 1):
@@ -544,6 +543,9 @@
                 for kind in range(2):
                     relay(0, 2, kind)
             if unit == 0 and at == 1:
+                for kind in range(2):
+                    for pair in needs(2):
+                        fan(*pair, kind)
                 arrive(0, 0, 1)
             if at == 2:
                 if unit == 0:
@@ -562,7 +564,7 @@
                 for pair in yields(unit - 1):
                     met(*pair).wait_recv()
                     push(*pair, False)
-            if at == 2 and unit > 1:
+            if at == 4 and unit > 1:
                 for pair in yields(unit - 2):
                     push(*pair, True)
             if at == 5 and b == 1:
@@ -577,7 +579,7 @@
                     for pair in yields(unit - 1):
                         push(*pair, True)
                     met(k, 0).wait_recv()
-                    push(k, 0, False)
+                    push(k, 0, False, True)
 
         compute(unit, ticks)
         if unit < last:
@@ -585,7 +587,9 @@
     for pair in yields(last):
         if pair[1] > 0:
             met(*pair).wait_recv()
-            push(*pair, False)
+            push(*pair, False, True)
+    for pair in yields(last):
+        push(*pair, False, False)
     for pair in yields(last):
         push(*pair, True)
     for unit in range(last + 1):

time: 50.6 us -> 50.5 us (level)
  no operation moved by 1% of the time
where the time goes in v5:
time: 50.5 us; the launch traced here: 50.3 us
  Pallas kernels  49.5 us (98%)
  between operations  0.8 us (2%)
    pallas_call x1, Pallas kernels, local(): pl.pallas_call(functools.partial(fused_kernel, groups, block), out_shape=...  47.1 us
    pallas_call x1, Pallas kernels, settle(): pl.pallas_call(settle_kernel, out_shape=tuple((jax.ShapeDtypeStruct(x.sha...  2.39 us

profile of v5, /device:TPU:0, one launch (start us, length us, event | category | flops | bytes accessed | tf_op | source)
XLA Modules:
  0.0 50.3 jit_solution(343208882494068751)
XLA Ops:
  0.6 47.1 %fused.1 = (bf16[2,48,4096]{2,1,0:T(8,128)(2,1)}, f32[2,48,512]{2,1,0:T(8,128)}, f32[2,48,512]{2,1,0:T(8,128)}, f32[32,512]{1,0:T(8,128)}, f32[32,512]{1,0:T(8,128)}) custom-call(s32[2]{0:T(128)} %lengths.1, bf16[32,512]{1,0:T(8,128)(2,1)} %pk.1, bf16[32,512]{1,0:T(8,128)(2,1)} %pv.1, bf16[2,48,512]{2,1,0:T(8,128)(2,1)} %rk.1, bf16[2,48,512]{2,1,0:T(8,128)(2,1)} %rv.1, ...), custom_call_target="tpu_custom_call" | custom-call | tf_op jit(solution)/shard_map/fused/pallas_call | solution.py:670
  47.8 2.4 %settle.1 = (f32[2,48,4096]{2,1,0:T(8,128)}, f32[2,48,512]{2,1,0:T(8,128)}, f32[2,48,512]{2,1,0:T(8,128)}, f32[32,512]{1,0:T(8,128)}, f32[32,512]{1,0:T(8,128)}) custom-call(bf16[2,48,4096]{2,1,0:T(8,128)(2,1)} %get-tuple-element.10.refs_0_, f32[2,48,512]{2,1,0:T(8,128)} %get-tuple-element.11.refs_1_, f32[2,48,512]{2,1,0:T(8,128)} %get-tuple-element.12.refs_2_, ...), custom_call_target="tpu_custom_call" | custom-call | tf_op jit(solution)/shard_map/settle/pallas_call | solution.py:641
